TPU v7x, 32 devices: a whole 2x2x4 slice. The times are simulated.
32 devices in a mesh: dp: 8 (over z, core), tensor: 4 (over y, x).
Axes of the slice: x: 2, y: 2, z: 4, core: 2. Of those that a mesh axis runs over, the one named last changes fastest.
Arguments:
- block_input: bfloat16 [16, 736, 1152], P('dp', 'tensor'), may hold values from -40 to 40
- key_mask: int32 [16, 736], P('dp'), may hold values from 0 to 1, as said below
- attn_norm_gain: float32 [1152], replicated, may hold values from 0.5 to 1.5
- attn_norm_bias: float32 [1152], replicated, may hold values from -1.5 to 1.5
- qkv_weight: bfloat16 [1152, 3, 1152], P('dp', None, 'tensor'), may hold values from -1.5 to 1.5
- qv_bias: float32 [2, 1152], P(None, 'tensor'), may hold values from -2.5 to 2.5
- out_weight: bfloat16 [1152, 1152], P('tensor', 'dp'), may hold values from -0.5 to 0.5
- out_bias: float32 [1152], replicated, may hold values from -2.5 to 2.5
- mlp_norm_gain: float32 [1152], replicated, may hold values from 0.5 to 1.5
- mlp_norm_bias: float32 [1152], replicated, may hold values from -1.5 to 1.5
- hidden_weight: bfloat16 [1152, 4304], P('dp', 'tensor'), may hold values from -0.1875 to 0.1875
- hidden_bias: float32 [4304], P('tensor'), may hold values from -2.5 to 2.5
- down_weight: bfloat16 [4304, 1152], P('tensor', 'dp'), may hold values from -0.125 to 0.125
- down_bias: float32 [1152], replicated, may hold values from -2.5 to 2.5
- grad_out: bfloat16 [16, 736, 1152], P('dp', 'tensor'), may hold values from -6 to 6
Outputs:
- block_output: bfloat16 [16, 736, 1152], P('dp', 'tensor')
- grad_input: float32 [16, 736, 1152], P('dp', 'tensor')
- grad_attn_norm_gain: float32 [1152], replicated
- grad_attn_norm_bias: float32 [1152], replicated
- grad_qkv_weight: float32 [1152, 3, 1152], P('dp', None, 'tensor')
- grad_qv_bias: float32 [2, 1152], P(None, 'tensor')
- grad_out_weight: float32 [1152, 1152], P('tensor', 'dp')
- grad_out_bias: float32 [1152], replicated
- grad_mlp_norm_gain: float32 [1152], replicated
- grad_mlp_norm_bias: float32 [1152], replicated
- grad_hidden_weight: float32 [1152, 4304], P('dp', 'tensor')
- grad_hidden_bias: float32 [4304], P('tensor')
- grad_down_weight: float32 [4304, 1152], P('tensor', 'dp')
- grad_down_bias: float32 [1152], replicated
Inputs may be any that keep to these rules, and one draw needn't show every extreme that they name: `key_mask`: each image's mask is 1 on its first L positions and 0 after them, with L from 368 to 729; some image has L = 729.
All inputs are finite; a program needn't handle non-finite values.
Results may differ from a plain program's by a relative error of at most 0.0095.
The roundings to bfloat16 on the way count: a program that leaves them out, or rounds other values in their place, can miss the bound.
Values may be sent and summed in bfloat16 or wider, within the bound.
A program may use at most 192 MiB of HBM per device.

v0:
```python
import functools
import math

import jax
import jax.numpy as jnp
from jax import lax
from jax.experimental import pallas as pl
from jax.experimental.pallas import tpu as pltpu
from jax.sharding import PartitionSpec as P

HD = 72
CHUNK = 768
F32 = jnp.float32
BF16 = jnp.bfloat16
LOG2E = math.log2(math.e)
NN = (((1,), (0,)), ((), ()))
NT = (((1,), (1,)), ((), ()))
TN = (((0,), (0,)), ((), ()))
MESH = pl.DeviceIdType.MESH
ANY = pl.BlockSpec(memory_space=pl.ANY)
VMEM = pl.BlockSpec(memory_space=pltpu.VMEM)
SMEM = pl.BlockSpec(memory_space=pltpu.SMEM)


layer_eps = 1e-06
gelu_root = math.sqrt(2.0 / math.pi)
gelu_cubic = 0.044715


def norm_stats(rows):
    center = rows - jnp.mean(rows, axis=-1, keepdims=True)
    inv_std = lax.rsqrt(jnp.mean(center * center, axis=-1, keepdims=True) + layer_eps)
    return (center * inv_std, inv_std)


def norm_forward(rows, gain, shift):
    unit, _ = norm_stats(rows)
    return (unit * gain + shift).astype(BF16)


def norm_backward(grad_normed, unit, inv_std, gain):
    scaled = grad_normed * gain
    return inv_std * (
        scaled
        - jnp.mean(scaled, axis=-1, keepdims=True)
        - unit * jnp.mean(scaled * unit, axis=-1, keepdims=True)
    )


def gelu_both(pre):
    tangent = jnp.tanh(gelu_root * (pre + gelu_cubic * pre * pre * pre))
    value = 0.5 * pre * (1.0 + tangent)
    slope = 0.5 * (1.0 + tangent) + 0.5 * pre * (1.0 - tangent * tangent) * gelu_root * (
        1.0 + 3.0 * gelu_cubic * pre * pre
    )
    return (value, slope)


def dot(a, b, dims=NN):
    return lax.dot_general(a, b, dims, preferred_element_type=F32)


def soft_columns(keys_in, queries, row_ok, factor):
    raw = jnp.where(row_ok, dot(keys_in, queries, NT), -1e30)
    top = jnp.max(raw, axis=0, keepdims=True)
    grown = jnp.exp2((raw - top) * factor)
    total = jnp.sum(grown, axis=0, keepdims=True)
    return grown * (1.0 / total)


def attend_forward_body(seq, heads, lens_ref, proj_ref, mixed_ref, qh, kh, vh, oh):
    width = heads * HD
    padded = qh.shape[1]
    for h in range(heads):
        qh[h, :seq] = proj_ref[0, :, h * HD : (h + 1) * HD]
        qh[h, seq:] = jnp.zeros((padded - seq, HD), BF16)
        kh[h] = proj_ref[0, :, width + h * HD : width + (h + 1) * HD]
        vh[h] = proj_ref[0, :, 2 * width + h * HD : 2 * width + (h + 1) * HD].T
    length = lens_ref[pl.program_id(0)]
    factor = HD**-0.5 * LOG2E

    def head(h, _):
        def chunk(c, _):
            row_ok = lax.broadcasted_iota(jnp.int32, (seq, CHUNK), 0) < length
            at = pl.ds(pl.multiple_of(c * CHUNK, CHUNK), CHUNK)
            probs = soft_columns(kh[h], qh[h, at], row_ok, factor)
            oh[h, at] = dot(vh[h], probs.astype(BF16)).T.astype(BF16)
            return 0

        return lax.fori_loop(0, padded // CHUNK, chunk, 0)

    lax.fori_loop(0, heads, head, 0)
    for h in range(heads):
        mixed_ref[0, :, h * HD : (h + 1) * HD] = oh[h, :seq]


def attend_forward(lens, proj):
    images, seq, triple = proj.shape
    heads = triple // (3 * HD)
    padded = -(-seq // CHUNK) * CHUNK
    return pl.pallas_call(
        functools.partial(attend_forward_body, seq, heads),
        out_shape=jax.ShapeDtypeStruct((images, seq, heads * HD), BF16),
        grid=(images,),
        in_specs=[SMEM, pl.BlockSpec((1, seq, triple), lambda i: (i, 0, 0))],
        out_specs=pl.BlockSpec((1, seq, heads * HD), lambda i: (i, 0, 0)),
        scratch_shapes=[
            pltpu.VMEM((heads, padded, HD), BF16),
            pltpu.VMEM((heads, seq, HD), BF16),
            pltpu.VMEM((heads, HD, seq), BF16),
            pltpu.VMEM((heads, padded, HD), BF16),
        ],
        name="attend_forward",
    )(lens, proj)


def attend_backward_body(
    seq, heads, lens_ref, proj_ref, gmix_ref, gproj_ref, gbias_ref, qh, kh, kt, vh, gh, gq, gk, gv
):
    width = heads * HD
    padded = qh.shape[1]
    for h in range(heads):
        qh[h, :seq] = proj_ref[0, :, h * HD : (h + 1) * HD]
        qh[h, seq:] = jnp.zeros((padded - seq, HD), BF16)
        gh[h, :seq] = gmix_ref[0, :, h * HD : (h + 1) * HD]
        gh[h, seq:] = jnp.zeros((padded - seq, HD), BF16)
        keys_in = proj_ref[0, :, width + h * HD : width + (h + 1) * HD]
        kh[h] = keys_in
        kt[h] = keys_in.T
        vh[h] = proj_ref[0, :, 2 * width + h * HD : 2 * width + (h + 1) * HD]
    length = lens_ref[pl.program_id(0)]
    scale = HD**-0.5
    factor = scale * LOG2E

    def head(h, _):
        gk[h] = jnp.zeros((seq, HD), F32)
        gv[h] = jnp.zeros((seq, HD), F32)

        def chunk(c, _):
            row_ok = lax.broadcasted_iota(jnp.int32, (seq, CHUNK), 0) < length
            at = pl.ds(pl.multiple_of(c * CHUNK, CHUNK), CHUNK)
            queries = qh[h, at]
            grads = gh[h, at]
            probs = soft_columns(kh[h], queries, row_ok, factor)
            grad_probs = dot(vh[h], grads, NT)
            gv[h] += dot(probs.astype(BF16), grads)
            delta = jnp.sum(probs * grad_probs, axis=0, keepdims=True)
            grad_scores = (probs * (grad_probs - delta) * scale).astype(BF16)
            gk[h] += dot(grad_scores, queries)
            gq[h, at] = dot(kt[h], grad_scores).T
            return 0

        return lax.fori_loop(0, padded // CHUNK, chunk, 0)

    lax.fori_loop(0, heads, head, 0)
    for h in range(heads):
        for c, held in enumerate((gq, gk, gv)):
            value = held[h, :seq]
            at = slice(c * width + h * HD, c * width + (h + 1) * HD)
            gproj_ref[0, :, at] = value.astype(BF16)
            gbias_ref[0, :, at] = jnp.sum(value, axis=0, keepdims=True)


def attend_backward(lens, proj, gmix):
    images, seq, triple = proj.shape
    heads = triple // (3 * HD)
    padded = -(-seq // CHUNK) * CHUNK
    return pl.pallas_call(
        functools.partial(attend_backward_body, seq, heads),
        out_shape=(
            jax.ShapeDtypeStruct((images, seq, triple), BF16),
            jax.ShapeDtypeStruct((images, 1, triple), F32),
        ),
        grid=(images,),
        in_specs=[
            SMEM,
            pl.BlockSpec((1, seq, triple), lambda i: (i, 0, 0)),
            pl.BlockSpec((1, seq, heads * HD), lambda i: (i, 0, 0)),
        ],
        out_specs=(
            pl.BlockSpec((1, seq, triple), lambda i: (i, 0, 0)),
            pl.BlockSpec((1, 1, triple), lambda i: (i, 0, 0)),
        ),
        scratch_shapes=[
            pltpu.VMEM((heads, padded, HD), BF16),
            pltpu.VMEM((heads, seq, HD), BF16),
            pltpu.VMEM((heads, HD, seq), BF16),
            pltpu.VMEM((heads, seq, HD), BF16),
            pltpu.VMEM((heads, padded, HD), BF16),
            pltpu.VMEM((heads, padded, HD), F32),
            pltpu.VMEM((heads, seq, HD), F32),
            pltpu.VMEM((heads, seq, HD), F32),
        ],
        name="attend_backward",
    )(lens, proj, gmix)


def plane():
    me = lax.axis_index("tensor")
    side = me + 1 - 2 * lax.rem(me, 2)
    over = lax.rem(me + 2, 4)
    return (me, side, over, lax.rem(side + 2, 4))


def greet(peers):
    barrier = pltpu.get_barrier_semaphore()
    for peer in peers:
        pl.semaphore_signal(barrier, inc=1, device_id={"tensor": peer}, device_id_type=MESH)
    pl.semaphore_wait(barrier, len(peers))


def greet_both(groups, side, over):
    row = lax.axis_index("dp")
    barrier = pltpu.get_barrier_semaphore()
    peers = [{"tensor": side}, {"tensor": over}, {"dp": row + 1 - 2 * lax.rem(row, 2)}]
    peers += [{"dp": lax.rem(row + 2 * k, groups)} for k in range(1, groups // 2)]
    for peer in peers:
        pl.semaphore_signal(barrier, inc=1, device_id=peer, device_id_type=MESH)
    pl.semaphore_wait(barrier, len(peers))


def remote(src, dst, send, recv, peer):
    return pltpu.make_async_remote_copy(
        src_ref=src,
        dst_ref=dst,
        send_sem=send,
        recv_sem=recv,
        device_id={"tensor": peer},
        device_id_type=MESH,
    )


def halves_of(rows):
    first = -(-rows // 32) * 16
    return (pl.ds(0, first), pl.ds(first, rows - first))


class Gather:
    def __init__(self, all_ref, rows, send, recv):
        me, side, over, _ = plane()
        low, high = halves_of(rows)
        plan = (
            (me, low, side),
            (me, high, over),
            (me, high, side),
            (me, low, over),
            (side, low, over),
            (over, high, side),
        )
        self.copies = []
        for k, (block, part, peer) in enumerate(plan):
            ref = all_ref.at[block, part]
            self.copies.append(remote(ref, ref, send.at[k], recv.at[k], peer))

    def start(self):
        for made in self.copies[:4]:
            made.start()

    def forward(self):
        for k in range(2):
            self.copies[k].wait_recv()
            self.copies[4 + k].start()

    def arrive(self):
        for made in self.copies[2:]:
            made.wait_recv()

    def finish(self):
        for made in self.copies:
            made.wait_send()


class Scatter:
    def __init__(self, part_ref, rows, near_ref, far_ref, pass_ref, send, recv):
        self.me, self.side, self.over, cross = plane()
        self.part_ref, self.near_ref, self.far_ref, self.pass_ref = part_ref, near_ref, far_ref, pass_ref
        self.halves = low, high = halves_of(rows)
        plan = (
            (part_ref.at[cross, low], near_ref.at[1, low], self.side),
            (part_ref.at[cross, high], near_ref.at[1, high], self.over),
            (part_ref.at[self.side, low], near_ref.at[0, low], self.side),
            (part_ref.at[self.over, high], near_ref.at[0, high], self.over),
            (pass_ref.at[low], far_ref.at[low], self.over),
            (pass_ref.at[high], far_ref.at[high], self.side),
        )
        self.copies = [remote(src, dst, send.at[k], recv.at[k], peer) for k, (src, dst, peer) in enumerate(plan)]

    def start(self):
        for made in self.copies[:4]:
            made.start()

    def forward(self):
        for k, (part, block) in enumerate(zip(self.halves, (self.over, self.side))):
            self.copies[k].wait_recv()
            mine = self.part_ref[block, part].astype(F32)
            self.pass_ref[part] = (mine + self.near_ref[1, part].astype(F32)).astype(BF16)
            self.copies[4 + k].start()

    def arrive(self):
        for made in self.copies[2:]:
            made.wait_recv()

    def total(self, rows):
        return (
            self.part_ref[self.me, rows].astype(F32)
            + self.near_ref[0, rows].astype(F32)
            + self.far_ref[rows].astype(F32)
        )

    def finish(self):
        for made in self.copies:
            made.wait_send()


STEPS = 6


def sems(*shape):
    return [pltpu.SemaphoreType.DMA(shape), pltpu.SemaphoreType.DMA(shape)]


def scatter_scratch(images, rows, width):
    return [
        pltpu.VMEM((images, 2, rows, width), BF16),
        pltpu.VMEM((images, rows, width), BF16),
        pltpu.VMEM((images, rows, width), BF16),
    ]


def params(cid):
    return pltpu.CompilerParams(collective_id=cid, has_side_effects=True, vmem_limit_bytes=60 << 20)


def lanes(width):
    return -(-width // 128) * 128


def pad_rows(rows):
    return -(-rows // 16) * 16


def clear_pads(ref, rows):
    full = ref.shape[1]
    for b in range(ref.shape[0]):
        ref[b, rows:full] = jnp.zeros((full - rows, ref.shape[2]), ref.dtype)


def at_row(ref):
    return ref[...].reshape(1, -1)


def for_image(i, images, act):
    for k in range(images):
        pl.when(i == k)(functools.partial(act, k))


def key_bias(mask, rows, full, seq):
    length = jnp.sum(mask.astype(F32), axis=1, keepdims=True).astype(jnp.int32)
    at = lax.broadcasted_iota(jnp.int32, (seq, 128 - HD), 0)
    lane = lax.broadcasted_iota(jnp.int32, (seq, 128 - HD), 1)
    block = sum((at >= b * full).astype(jnp.int32) for b in range(1, seq // full))
    inner = at - block * full
    good = (inner < rows) & (inner + block * rows < length)
    bias = jnp.where(good, 0.0, -1e30)
    ones = jnp.where(lane == 0, 1.0, 0.0)
    return (jnp.where(lane == 0, bias, 0.0).astype(BF16), ones.astype(BF16))


def soft_open(keys_in, queries, factor):
    raw = dot(keys_in, queries, NT)
    top = jnp.max(raw, axis=0, keepdims=True)
    grown = jnp.exp2((raw - top) * factor)
    total = jnp.sum(grown, axis=0, keepdims=True)
    return grown * (1.0 / total)


def over_dp(src, dst, send, recv, peer):
    return pltpu.make_async_remote_copy(
        src_ref=src, dst_ref=dst, send_sem=send, recv_sem=recv, device_id={"dp": peer}, device_id_type=MESH
    )


class Spread:
    def __init__(self, groups, all_ref, send, recv):
        row = lax.axis_index("dp")
        twin = row + 1 - 2 * lax.rem(row, 2)
        half = groups // 2
        chip = lax.div(row, 2)
        self.relayed = half == 4
        self.out, self.back = [], []
        for k in range(half):
            came = all_ref.at[lax.rem(row + groups - 2 * k, groups)]
            self.back.append(over_dp(came, came, send.at[half + k], recv.at[half + k], twin))
            if k > 0:
                mine = all_ref.at[row]
                self.out.append(over_dp(mine, mine, send.at[k], recv.at[k], lax.rem(row + 2 * k, groups)))
        self.asked = {}
        if self.relayed:
            self.asked = {0: chip != 3, 2: chip != 0}
            self.inner = (chip == 1) | (chip == 2)
            up = lax.div(chip, 2)
            came = all_ref.at[lax.rem(row + 4, groups)]
            self.relay = over_dp(came, came, send.at[0], recv.at[1 + 2 * up], row + 4 * up - 2)

    def where(self, k, act):
        if k in self.asked:
            pl.when(self.asked[k])(act)
        else:
            act()

    def start(self):
        for k in (1, 0, 2) if self.relayed else range(len(self.out)):
            self.where(k, self.out[k].start)
        self.back[0].start()

    def hop(self):
        if self.relayed:
            self.out[1].wait_recv()
            pl.when(self.inner)(self.relay.start)
            self.back[2].start()

    def forward(self):
        for k, (far, near) in enumerate(zip(self.out, self.back[1:])):
            if k != 1 or not self.relayed:
                far.wait_recv()
                near.start()

    def arrive(self):
        for made in self.back:
            made.wait_recv()

    def finish(self):
        for k, made in enumerate(self.out):
            self.where(k, made.wait_send)
        for made in self.back:
            made.wait_send()
        if self.relayed:
            pl.when(self.inner)(self.relay.wait_send)


class Moves:
    def __init__(self, sem):
        self.sem, self.made = sem, []

    def plan(self, src, dst):
        made = pltpu.make_async_copy(src, dst, self.sem.at[len(self.made)])
        self.made.append(made)
        return made

    def start(self, src, dst):
        made = self.plan(src, dst)
        made.start()
        return made

    def finish(self):
        for made in self.made:
            made.wait()


def front_body(
    groups, rows, heads,
    x_ref, grad_ref, mask_ref, gain_one, bias_one, bias_out, gain_two, bias_two, qv_ref, wq_ref, wo_ref, wh_ref, wd_ref,
    one_out, full_out, two_out, hidden_out, qh_out, kh_out, vh_out, mixed_out, wq_out, wo_out, wh_out, wd_out,
    one_ref, full_ref, two_ref, hidden_ref, qh, kh, vh, mixed_ref, wq_all, wo_all, wh_all, wd_all,
    oh, part_ref, near, far, passing, osem,
    asend, arecv, fsend, frecv, ssend, srecv, gsend, grecv, wsend, wrecv,
):
    images = x_ref.shape[0]
    full = one_ref.shape[2]
    seq = 4 * full
    width = heads * HD
    me, side, over, _ = plane()
    mine = lax.axis_index("dp")
    wq_all[mine, :, 3 * width :] = jnp.zeros_like(wq_all[mine, :, 3 * width :])
    for c in range(3):
        wq_all[mine, :, c * width : (c + 1) * width] = wq_ref[c]
    weights = [Spread(groups, wq_all, wsend.at[0], wrecv.at[0])]
    for k, (own, everyone) in enumerate(((wo_ref, wo_all), (wh_ref, wh_all), (wd_ref, wd_all))):
        count = own.shape[1]
        everyone[mine, :, count:] = jnp.zeros_like(everyone[mine, :, count:])
        everyone[mine, :, :count] = own[...]
        weights.append(Spread(groups, everyone, wsend.at[k + 1], wrecv.at[k + 1]))
    wq, wo, wh, wd = weights
    ones, sums, twos = [], [], []
    for i in range(images):
        clear_pads(one_ref.at[i], rows)
        clear_pads(two_ref.at[i], rows)
        ones.append(Gather(one_ref.at[i], rows, asend.at[i], arecv.at[i]))
        sums.append(Scatter(part_ref.at[i], rows, near.at[i], far.at[i], passing.at[i], ssend.at[i], srecv.at[i]))
        twos.append(Gather(two_ref.at[i], rows, gsend.at[i], grecv.at[i]))
    mixed_ref[:, :, :, width:] = jnp.zeros_like(mixed_ref[:, :, :, width:])
    clear_pads(full_ref, rows)
    grads = Gather(full_ref, rows, fsend, frecv)
    stores = Moves(osem)
    put_weight = [stores.plan(a, b) for a, b in ((wq_all, wq_out), (wo_all, wo_out), (wh_all, wh_out), (wd_all, wd_out))]
    put_full = stores.plan(full_ref, full_out)
    pairs = (
        (one_ref, one_out), (two_ref, two_out), (hidden_ref, hidden_out), (qh, qh_out), (kh, kh_out), (vh, vh_out),
        (mixed_ref, mixed_out),
    )
    put = [[stores.plan(a.at[i], b.at[i]) for a, b in pairs] for i in range(images)]

    def enter(i):
        one_ref[i, me, :rows] = norm_forward(x_ref[i].astype(F32), at_row(gain_one), at_row(bias_one))

    enter(0)
    greet_both(groups, side, over)
    ones[0].start()
    wq.start()
    for i in range(1, images):
        enter(i)
        ones[i].start()
    wo.start()
    wh.start()
    wd.start()
    full_ref[me, :rows] = grad_ref[0]
    for i in range(images):
        bias, tail = key_bias(mask_ref[i : i + 1], rows, full, seq)
        for h in range(heads):
            kh[i, h, :, HD:] = bias
            vh[i, h, :, HD:] = jnp.zeros_like(bias)
            qh[i, h, :, HD:] = tail
    for step in ones:
        step.forward()
    grads.start()
    wq.hop()
    wq.forward()
    factor = HD**-0.5 * LOG2E
    shift_q, shift_v = qv_ref[0:1], qv_ref[1:2]

    def project(i):
        weight = wq_all[:, :, : 3 * width].reshape(-1, 3 * width)

        def block(b, _):
            at = pl.ds(pl.multiple_of(b * full, 16), full)
            value = dot(one_ref[i, b], weight)
            queries = (value[:, :width] + shift_q).astype(BF16)
            keys_in = value[:, width : 2 * width].astype(BF16)
            values = (value[:, 2 * width :] + shift_v).astype(BF16)
            for h in range(heads):
                here = slice(h * HD, (h + 1) * HD)
                qh[i, h, at, :HD] = queries[:, here]
                kh[i, h, at, :HD] = keys_in[:, here]
                vh[i, h, at, :HD] = values[:, here]
            return 0

        lax.fori_loop(0, 4, block, 0)

    def attend(i):
        def head(h, _):
            probs = soft_open(kh[i, h], qh[i, h], factor)
            oh[h] = dot(vh[i, h, :, :HD].T, probs.astype(BF16)).T.astype(BF16)
            return 0

        lax.fori_loop(0, heads, head, 0, unroll=2)
        for h in range(heads):
            for b in range(4):
                mixed_ref[i, b, :, h * HD : (h + 1) * HD] = oh[h, b * full : (b + 1) * full]

    def combine(i):
        weight = wo_all[:, :, :width].reshape(-1, width)

        def block(b, _):
            part_ref[i, b] = dot(mixed_ref[i, b, :, :width], weight, NT).astype(BF16)
            return 0

        lax.fori_loop(0, 4, block, 0)

    def ready(k):
        ones[k].arrive()
        put[k][0].start()
        if k == 0:
            wq.arrive()
            put_weight[0].start()

    def between(k):
        for made in put[k][3:]:
            made.start()
        if k == 0:
            grads.forward()
            wo.hop()
            wo.forward()
            wh.hop()
            wo.arrive()
            put_weight[1].start()

    def send(k):
        if k > 0:
            sums[k - 1].forward()
        sums[k].start()

    def image(i, _):
        for_image(i, images, ready)
        project(i)
        attend(i)
        for_image(i, images, between)
        combine(i)
        for_image(i, images, send)
        return 0

    lax.fori_loop(0, images, image, 0)

    def settle(i):
        sums[i].arrive()
        hidden = x_ref[i].astype(F32) + sums[i].total(pl.ds(0, rows)) + at_row(bias_out)
        hidden_ref[i] = hidden
        two_ref[i, me, :rows] = norm_forward(hidden, at_row(gain_two), at_row(bias_two))
        twos[i].start()
        put[i][2].start()

    for i in range(images - 1):
        settle(i)
    sums[-1].forward()
    wd.hop()
    for i in range(images - 1):
        twos[i].forward()
    settle(images - 1)
    grads.arrive()
    put_full.start()
    wh.forward()
    twos[-1].forward()
    wh.arrive()
    put_weight[2].start()
    wd.forward()
    for i in range(images):
        twos[i].arrive()
        put[i][1].start()
    wd.arrive()
    put_weight[3].start()
    for step in ones + sums + twos + weights + [grads]:
        step.finish()
    stores.finish()


def front(groups, block_input, grad_out, key_mask, vectors, qv_bias, wq, wo, wh, wd):
    images, rows, model = block_input.shape
    full = pad_rows(rows)
    width = wo.shape[1]
    units = wh.shape[1]
    heads = width // HD
    seq = 4 * full
    depth = wo.shape[0]
    held = [
        ((images, 4, full, model), BF16),
        ((4, full, model), BF16),
        ((images, 4, full, model), BF16),
        ((images, rows, model), F32),
        ((images, heads, seq, 128), BF16),
        ((images, heads, seq, 128), BF16),
        ((images, heads, seq, 128), BF16),
        ((images, 4, full, lanes(width)), BF16),
        ((groups, depth, lanes(3 * width)), BF16),
        ((groups, depth, lanes(width)), BF16),
        ((groups, depth, lanes(units)), BF16),
        ((groups, depth, lanes(units)), BF16),
    ]
    return pl.pallas_call(
        functools.partial(front_body, groups, rows, heads),
        out_shape=tuple(jax.ShapeDtypeStruct(*h) for h in held),
        in_specs=[VMEM] * 13,
        out_specs=(ANY,) * len(held),
        scratch_shapes=[pltpu.VMEM(*h) for h in held]
        + [pltpu.VMEM((heads, seq, HD), BF16), pltpu.VMEM((images, 4, full, model), BF16)]
        + scatter_scratch(images, full, model)
        + [pltpu.SemaphoreType.DMA((7 * images + 5,))]
        + sems(images, STEPS)
        + sems(STEPS)
        + sems(images, STEPS) * 2
        + sems(4, groups),
        compiler_params=params(0),
        name="front",
    )(block_input, grad_out, key_mask, *vectors, qv_bias, wq, wo, wh, wd)


class Reduce:
    def __init__(self, groups, grad_ref, twin_ref, far_ref, tsend, trecv, fsend, frecv):
        self.grad_ref, self.twin_ref, self.far_ref = grad_ref, twin_ref, far_ref
        depth = grad_ref.shape[0] // groups
        rows = lambda block: pl.ds(pl.multiple_of(block * depth, 16), depth)
        row = lax.axis_index("dp")
        core = lax.rem(row, 2)
        self.slot, self.mine = lax.div(row, 2), rows(row)
        self.near, self.away = [], []
        for k in range(groups // 2):
            theirs = grad_ref.at[rows(2 * k + 1 - core)]
            self.near.append(over_dp(theirs, twin_ref.at[k], tsend.at[k], trecv.at[k], row + 1 - 2 * core))
        for k in range(1, groups // 2):
            peer = lax.rem(row + 2 * k, groups)
            slot = lax.div(peer, 2)
            made = over_dp(twin_ref.at[slot], far_ref.at[k - 1], fsend.at[k], frecv.at[k], peer)
            self.away.append((slot, rows(peer), made))

    def start(self):
        for made in self.near:
            made.start()

    def pair(self):
        for made in self.near:
            made.wait_recv()
        for slot, part, made in self.away:
            mine = self.grad_ref[part].astype(F32)
            self.twin_ref[slot] = (self.twin_ref[slot].astype(F32) + mine).astype(BF16)
            made.start()

    def total(self):
        value = self.twin_ref[self.slot].astype(F32) + self.grad_ref[self.mine].astype(F32)
        for k, (_, _, made) in enumerate(self.away):
            made.wait_recv()
            value = value + self.far_ref[k].astype(F32)
        return value

    def finish(self):
        for made in self.near + [made for _, _, made in self.away]:
            made.wait_send()


def reduce_scratch(groups, depth, width):
    half, width = groups // 2, lanes(width)
    return [pltpu.VMEM((half, depth, width), BF16), pltpu.VMEM((half - 1, depth, width), BF16)] + sems(half) * 2


def outer(out_ref, left_ref, right_ref, width):
    images, blocks, full, model = left_ref.shape
    count = images * blocks * full
    tile = 384
    if out_ref.shape[1] > width:
        out_ref[:, width:] = jnp.zeros_like(out_ref[:, width:])

    def part(c, _):
        at = pl.ds(pl.multiple_of(c * tile, tile), tile)
        left = left_ref[:, :, :, at].reshape(count, tile)
        right = right_ref[:, :, :, :width].reshape(count, width)
        out_ref[at, :width] = dot(left, right, TN).astype(BF16)
        return 0

    lax.fori_loop(0, model // tile, part, 0)


def turn_body(
    groups, rows,
    two_hbm, full_hbm, wh_hbm, wd_hbm, hidden_hbm, grad_ref, gain_ref, hb_ref,
    glow_hbm, ghid_hbm, gwh_hbm, mpart_hbm, gwd_ref, sums_ref, hsum_ref,
    two_ref, wh_ref, wd_ref, hidden_ref, glow_ref, ghid_ref, gwh_ref, mpart_ref,
    full_ref, act_ref, gpl_ref, gpart_ref, gwd_part, lsem, osem,
    near, far, passing, twin, away, tsend, trecv, fsend, frecv, ssend, srecv, gsend, grecv, asend, arecv,
):
    images, _, full, model = two_ref.shape
    units = hb_ref.shape[0]
    me, side, over, _ = plane()
    loads, stores = Moves(lsem), Moves(osem)
    got = [[loads.start(two_hbm.at[0], two_ref.at[0])]]
    got[0].append(loads.start(wh_hbm, wh_ref))
    got[0].append(loads.start(full_hbm, full_ref.at[0]))
    got[0].append(loads.start(wd_hbm, wd_ref))
    for i in range(1, images):
        got.append([loads.start(two_hbm.at[i], two_ref.at[i])])
    got_hidden = loads.start(hidden_hbm, hidden_ref)
    put_mpart = [stores.plan(mpart_ref.at[i], mpart_hbm.at[i]) for i in range(images)]
    put_ghid = [stores.plan(ghid_ref.at[i], ghid_hbm.at[i]) for i in range(images)]
    put_glow = [stores.plan(glow_ref.at[i], glow_hbm.at[i]) for i in range(images)]
    put_gwh = stores.plan(gwh_ref, gwh_hbm)
    hsum_ref[...] = jnp.zeros_like(hsum_ref)
    sums, gathers, grads = [], [], [None]
    for i in range(images):
        clear_pads(glow_ref.at[i], rows)
        sums.append(Scatter(gpart_ref.at[i], rows, near.at[i], far.at[i], passing.at[i], ssend.at[i], srecv.at[i]))
        gathers.append(Gather(glow_ref.at[i], rows, gsend.at[i], grecv.at[i]))
        if i > 0:
            clear_pads(full_ref.at[i], rows)
            full_ref[i, me, :rows] = grad_ref[i]
            grads.append(Gather(full_ref.at[i], rows, asend.at[i], arecv.at[i]))
    down = Reduce(groups, gwd_part, twin, away, tsend, trecv, fsend, frecv)
    greet_both(groups, side, over)
    for step in grads[1:]:
        step.start()
    wide = lambda ref: ref[:, :, :units].reshape(model, units)
    shift = at_row(hb_ref)

    def ascend(i):
        def pair(c, _):
            at = pl.ds(2 * c, 2)
            pre = dot(two_ref[i, at].reshape(2 * full, model), wide(wh_ref)) + shift
            value, slope = gelu_both(pre)
            act_ref[i, at] = value.astype(BF16).reshape(2, full, units)
            grad_pre = dot(full_ref[i, at].reshape(2 * full, model), wide(wd_ref)) * slope
            hsum_ref[...] += jnp.sum(grad_pre, axis=0, keepdims=True)
            low = grad_pre.astype(BF16)
            gpl_ref[i, at] = low.reshape(2, full, units)
            gpart_ref[i, at] = dot(low, wide(wh_ref), NT).astype(BF16).reshape(2, full, model)
            return 0

        lax.fori_loop(0, 2, pair, 0)

    def descend(k, _):
        at = pl.ds(2 * lax.rem(k, 2), 2)
        i = lax.div(k, 2)
        part = dot(act_ref[i, at].reshape(2 * full, units), wide(wd_ref), NT)
        mpart_ref[i, at] = part.astype(BF16).reshape(2, full, model)
        return 0

    totals = [0.0, 0.0, 0.0, 0.0]

    def settle(i):
        sums[i].arrive()
        grad_normed = sums[i].total(pl.ds(0, rows))
        unit, inv_std = norm_stats(hidden_ref[i])
        upper = full_ref[i, me, :rows].astype(F32)
        grad_hidden = upper + norm_backward(grad_normed, unit, inv_std, at_row(gain_ref))
        ghid_ref[i] = grad_hidden
        glow_ref[i, me, :rows] = grad_hidden.astype(BF16)
        gathers[i].start()
        put_ghid[i].start()
        for k, term in enumerate((grad_normed * unit, grad_normed, grad_hidden, upper)):
            totals[k] = totals[k] + jnp.sum(term, axis=0, keepdims=True)

    def ready(k):
        for made in got[k]:
            made.wait()
        if k > 0:
            grads[k].arrive()

    def send(k):
        if k == 0:
            for step in grads[1:]:
                step.forward()
        if k > 0:
            sums[k - 1].forward()
        sums[k].start()

    def image(i, _):
        for_image(i, images, ready)
        ascend(i)
        for_image(i, images, send)
        return 0

    lax.fori_loop(0, images, image, 0)
    outer(gwd_part, full_ref, act_ref, units)
    down.start()
    got_hidden.wait()
    for i in range(images - 1):
        settle(i)
    sums[-1].forward()
    down.pair()
    outer(gwh_ref, two_ref, gpl_ref, units)
    put_gwh.start()
    for i in range(images - 1):
        gathers[i].forward()
    settle(images - 1)
    lax.fori_loop(0, 2 * images, descend, 0)
    for made in put_mpart:
        made.start()
    gathers[-1].forward()
    for k in range(4):
        sums_ref[k : k + 1] = totals[k]
    gwd_ref[...] = down.total()[:, :units]
    for i in range(images):
        gathers[i].arrive()
        put_glow[i].start()
    for step in sums + gathers + grads[1:] + [down]:
        step.finish()
    stores.finish()


def turn(groups, rows, two, full_grad, wh, wd, hidden, grad_out, gain, bias):
    images, _, full, model = two.shape
    units = bias.shape[0]
    depth = model // groups
    blocks = ((images, 4, full, model), BF16)
    wide = ((images, 4, full, units), BF16)
    outs = [blocks, ((images, rows, model), F32), ((model, lanes(units)), BF16), blocks]
    ins = [blocks, (wh.shape, BF16), (wh.shape, BF16), (hidden.shape, F32)]
    more = [((depth, units), F32), ((4, model), F32), ((1, units), F32)]
    return pl.pallas_call(
        functools.partial(turn_body, groups, rows),
        out_shape=tuple(jax.ShapeDtypeStruct(*h) for h in outs + more),
        in_specs=[ANY] * 5 + [VMEM] * 3,
        out_specs=(ANY,) * 4 + (VMEM,) * 3,
        scratch_shapes=[pltpu.VMEM(*h) for h in ins + outs + [blocks, wide, wide, blocks, ((model, lanes(units)), BF16)]]
        + [pltpu.SemaphoreType.DMA((images + 4,)), pltpu.SemaphoreType.DMA((3 * images + 1,))]
        + scatter_scratch(images, full, model)
        + reduce_scratch(groups, depth, units)
        + sems(images, STEPS) * 3,
        compiler_params=params(1),
        name="turn",
    )(two, full_grad, wh, wd, hidden, grad_out, gain, bias)


def close_body(
    groups, rows, heads,
    glow_hbm, mixed_hbm, gwh_hbm, mpart_hbm, wo_hbm, qh_hbm, kh_hbm, vh_hbm, wq_hbm, hidden_hbm, ghid_hbm, x_hbm, one_hbm,
    gain_ref, bias_ref, tsum_ref, hsum_ref,
    out_ref, gin_ref, gwq_ref, gwo_ref, gwh_ref, both_ref,
    tok, mixed_ref, gwh_part, mpart_ref, wo_ref, qh, kh, vh, wq_ref, hidden_ref, ghid_ref, x_ref,
    gq, gk, gv, gh, bsum, gproj, npart, gwq_part, gwo_part, lsem,
    near, far, passing, near2, far2, passing2,
    htwin, haway, htsend, htrecv, hfsend, hfrecv,
    otwin, oaway, otsend, otrecv, ofsend, ofrecv,
    qtwin, qaway, qtsend, qtrecv, qfsend, qfrecv,
    mid, msend, mrecv, ssend, srecv, vsend, vrecv, twin_in, far_in, side_in, over_in,
):
    images, _, full, model = tok.shape
    width = heads * HD
    seq = 4 * full
    me, side, over, _ = plane()
    mine = lax.axis_index("dp")
    loads = Moves(lsem)
    held = (
        (glow_hbm, tok), (mixed_hbm, mixed_ref), (gwh_hbm, gwh_part), (mpart_hbm, mpart_ref), (wo_hbm, wo_ref),
        (qh_hbm, qh), (kh_hbm, kh), (vh_hbm, vh), (wq_hbm, wq_ref), (hidden_hbm, hidden_ref), (ghid_hbm, ghid_ref),
        (x_hbm, x_ref),
    )
    got = [loads.start(src, dst) for src, dst in held]
    got_one = loads.plan(one_hbm, tok)
    bsum[...] = jnp.zeros_like(bsum)
    outs, sums = [], []
    for i in range(images):
        outs.append(Scatter(mpart_ref.at[i], rows, near2.at[i], far2.at[i], passing2.at[i], msend.at[i], mrecv.at[i]))
        sums.append(Scatter(npart.at[i], rows, near.at[i], far.at[i], passing.at[i], ssend.at[i], srecv.at[i]))
    red_h = Reduce(groups, gwh_part, htwin, haway, htsend, htrecv, hfsend, hfrecv)
    red_o = Reduce(groups, gwo_part, otwin, oaway, otsend, otrecv, ofsend, ofrecv)
    red_q = Reduce(groups, gwq_part, qtwin, qaway, qtsend, qtrecv, qfsend, qfrecv)
    greet_both(groups, side, over)
    for made in got[:4]:
        made.wait()
    red_h.start()
    for step in outs:
        step.start()
    outer(gwo_part, tok, mixed_ref, width)
    red_o.start()
    got[4].wait()

    def mix(i, _):
        value = dot(tok[i].reshape(seq, model), wo_ref[:, :, :width].reshape(model, width)).astype(BF16)
        for h in range(heads):
            gh[i, h] = value[:, h * HD : (h + 1) * HD]
        return 0

    lax.fori_loop(0, images, mix, 0)
    got_one.start()
    red_h.pair()
    outs[0].forward()
    red_o.pair()
    for made in got[5:]:
        made.wait()
    scale = HD**-0.5

    def attend(i):
        def head(h, _):
            queries = qh[i, h]
            grads = gh[i, h]
            keys_in = kh[i, h]
            probs = soft_open(keys_in, queries, scale * LOG2E)
            grad_probs = dot(vh[i, h, :, :HD], grads, NT)
            grad_values = dot(probs.astype(BF16), grads)
            delta = jnp.sum(probs * grad_probs, axis=0, keepdims=True)
            grad_scores = (probs * (grad_probs - delta) * scale).astype(BF16)
            grad_keys = dot(grad_scores, queries[:, :HD])
            grad_queries = dot(keys_in[:, :HD].T, grad_scores).T
            for c, (held, value) in enumerate(((gq, grad_queries), (gk, grad_keys), (gv, grad_values))):
                held[h] = value.astype(BF16)
                bsum[h, c : c + 1] += jnp.sum(value, axis=0, keepdims=True)
            return 0

        lax.fori_loop(0, heads, head, 0, unroll=4)
        for h in range(heads):
            for c, held in enumerate((gq, gk, gv)):
                at = slice(c * width + h * HD, c * width + (h + 1) * HD)
                for b in range(4):
                    gproj[i, b, :, at] = held[h, b * full : (b + 1) * full]

    def spread(i):
        def pair(c, _):
            at = pl.ds(2 * c, 2)
            part = dot(gproj[i, at].reshape(2 * full, 3 * width), wq_ref[:, :, : 3 * width].reshape(model, 3 * width), NT)
            npart[i, at] = part.astype(BF16).reshape(2, full, model)
            return 0

        lax.fori_loop(0, 2, pair, 0)

    def between(k):
        if k == 0:
            for step in outs[1:]:
                step.forward()

    def send(k):
        if k > 0:
            sums[k - 1].forward()
        sums[k].start()

    def image(i, _):
        attend(i)
        for_image(i, images, between)
        spread(i)
        for_image(i, images, send)
        return 0

    lax.fori_loop(0, images, image, 0)
    got_one.wait()
    outer(gwq_part, tok, gproj, 3 * width)
    red_q.start()
    totals = [0.0, 0.0]

    def settle(i):
        sums[i].arrive()
        grad_normed = sums[i].total(pl.ds(0, rows))
        unit, inv_std = norm_stats(x_ref[i].astype(F32))
        gin_ref[i] = ghid_ref[i] + norm_backward(grad_normed, unit, inv_std, at_row(gain_ref))
        for k, term in enumerate((grad_normed * unit, grad_normed)):
            totals[k] = totals[k] + jnp.sum(term, axis=0, keepdims=True)

    for i in range(images - 1):
        settle(i)
    red_q.pair()
    sums[-1].forward()
    for i in range(images):
        outs[i].arrive()
        out_ref[i] = (hidden_ref[i] + outs[i].total(pl.ds(0, rows)) + at_row(bias_ref)).astype(BF16)
    gwh_ref[...] = red_h.total()[:, : gwh_ref.shape[1]]
    gwo_ref[...] = red_o.total()[:, :width]
    settle(images - 1)

    mid[0] = jnp.zeros_like(mid[0])
    mid[0, 0:4] = tsum_ref[...]
    for k in range(2):
        mid[0, 4 + k : 5 + k] = totals[k]
    for h in range(heads):
        for c in range(3):
            mid[0, 6:7, c * width + h * HD : c * width + (h + 1) * HD] = bsum[h, c : c + 1]
    mid[0, 7:8, : hsum_ref.shape[1]] = hsum_ref[...]
    half = groups // 2
    place = lax.div(mine, 2)
    twin = over_dp(mid.at[0], twin_in, vsend.at[0], vrecv.at[0], mine + 1 - 2 * lax.rem(mine, 2))
    twin.start()
    twin.wait()
    mid[1] = mid[0] + twin_in[...]
    far_in[place] = mid[1]
    aways = []
    for k in range(1, half):
        peer = lax.rem(mine + 2 * k, groups)
        aways.append(over_dp(mid.at[1], far_in.at[place], vsend.at[k], vrecv.at[k], peer))
        aways[-1].start()
    for made in aways:
        made.wait()
    held = far_in[0]
    for k in range(1, half):
        held = held + far_in[k]
    mid[2] = held
    near_sum = remote(mid.at[2], side_in, vsend.at[half], vrecv.at[half], side)
    near_sum.start()
    near_sum.wait()
    mid[3] = mid[2] + side_in[...]
    over_sum = remote(mid.at[3], over_in, vsend.at[half + 1], vrecv.at[half + 1], over)
    over_sum.start()
    over_sum.wait()
    both_ref[0:6] = mid[3, 0:6] + over_in[0:6]
    both_ref[6:8] = mid[2, 6:8]
    total = red_q.total()
    for c in range(3):
        gwq_ref[c] = total[:, c * width : (c + 1) * width]
    for step in sums + outs + [red_h, red_o, red_q]:
        step.finish()


def close(groups, rows, heads, held, one, gain, bias, tsum, hsum):
    images, _, full, model = held[0].shape
    width = heads * HD
    units = hsum.shape[1]
    depth = model // groups
    seq = 4 * full
    piece = pltpu.VMEM((heads, seq, HD), BF16)
    small = pltpu.VMEM((8, model), F32)
    return pl.pallas_call(
        functools.partial(close_body, groups, rows, heads),
        out_shape=(
            jax.ShapeDtypeStruct((images, rows, model), BF16),
            jax.ShapeDtypeStruct((images, rows, model), F32),
            jax.ShapeDtypeStruct((3, depth, width), F32),
            jax.ShapeDtypeStruct((depth, width), F32),
            jax.ShapeDtypeStruct((depth, units), F32),
            jax.ShapeDtypeStruct((8, model), F32),
        ),
        in_specs=[ANY] * 13 + [VMEM] * 4,
        out_specs=(VMEM,) * 6,
        scratch_shapes=[pltpu.VMEM(h.shape, h.dtype) for h in held]
        + [piece] * 3
        + [
            pltpu.VMEM((images, heads, seq, HD), BF16),
            pltpu.VMEM((heads, 3, HD), F32),
            pltpu.VMEM((images, 4, full, 3 * width), BF16),
            pltpu.VMEM((images, 4, full, model), BF16),
            pltpu.VMEM((model, lanes(3 * width)), BF16),
            pltpu.VMEM((model, lanes(width)), BF16),
            pltpu.SemaphoreType.DMA((13,)),
        ]
        + scatter_scratch(images, full, model) * 2
        + reduce_scratch(groups, depth, units)
        + reduce_scratch(groups, depth, width)
        + reduce_scratch(groups, depth, 3 * width)
        + [pltpu.VMEM((4, 8, model), F32)]
        + sems(images, STEPS) * 2
        + sems(groups // 2 + 2)
        + [small, pltpu.VMEM((groups // 2, 8, model), F32), small, small],
        compiler_params=params(2),
        name="close",
    )(*held, one, gain, bias, tsum, hsum)


def deliver_body(width, out, gin, gwq, gwo, gwh, gwd, both, *refs):
    refs, sem = refs[:-1], refs[-1]
    loads = Moves(sem)
    for src, dst in zip((out, gin, gwq, gwo, gwh, gwd), refs):
        loads.start(src, dst)
    qv, unit = refs[6:8]
    qv[0:1] = both[6:7, :width]
    qv[1:2] = both[6:7, 2 * width : 3 * width]
    unit[...] = both[7, : unit.shape[0]]
    for k, dst in enumerate(refs[8:]):
        dst[...] = both[k]
    loads.finish()


def deliver(width, units, out, gin, gwq, gwo, gwh, gwd, both):
    model = both.shape[1]
    same = [jax.ShapeDtypeStruct(v.shape, v.dtype) for v in (out, gin, gwq, gwo, gwh, gwd)]
    more = [jax.ShapeDtypeStruct(dims, F32) for dims in ((2, width), (units,)) + ((model,),) * 6]
    return pl.pallas_call(
        functools.partial(deliver_body, width),
        out_shape=tuple(same + more),
        in_specs=[ANY] * 6 + [VMEM],
        out_specs=(VMEM,) * 14,
        scratch_shapes=[pltpu.SemaphoreType.DMA((6,))],
        compiler_params=pltpu.CompilerParams(vmem_limit_bytes=60 << 20),
        name="deliver",
    )(out, gin, gwq, gwo, gwh, gwd, both)


def gather_rows(rows):
    return lax.all_gather(rows, "tensor", axis=1, tiled=True)


def scatter_rows(part):
    return lax.psum_scatter(part, "tensor", scatter_dimension=1, tiled=True).astype(F32)


def shards(
    groups,
    ranks,
    block_input,
    key_mask,
    attn_norm_gain,
    attn_norm_bias,
    qkv_weight,
    qv_bias,
    out_weight,
    out_bias,
    mlp_norm_gain,
    mlp_norm_bias,
    hidden_weight,
    hidden_bias,
    down_weight,
    down_bias,
    grad_out,
):
    flat = ranks == 4
    images, rows, model = block_input.shape
    seq = key_mask.shape[1]
    width = qkv_weight.shape[2]
    units = hidden_weight.shape[1]

    def weight(shard):
        return lax.all_gather(shard, "dp", axis=0, tiled=True)

    def owned(grad):
        return lax.psum_scatter(grad.astype(BF16), "dp", scatter_dimension=0, tiled=True).astype(F32)

    out_rows, down_rows = out_weight.T, down_weight.T
    if flat:
        (
            normed_one, grad_full, normed_two, hidden_res, qh, kh, vh, mixed, qkv_all, out_all, hidden_all, down_all
        ) = front(
            groups,
            block_input,
            grad_out,
            key_mask,
            (attn_norm_gain, attn_norm_bias, out_bias, mlp_norm_gain, mlp_norm_bias),
            qv_bias,
            qkv_weight.transpose(1, 0, 2),
            out_rows,
            hidden_weight,
            down_rows,
        )
        hidden_full, grad_hidden, hidden_part, mpart, grad_down_w, mlp_sums, unit_sums = turn(
            groups, rows, normed_two, grad_full, hidden_all, down_all, hidden_res, grad_out, mlp_norm_gain, hidden_bias
        )
        held = (
            hidden_full, mixed, hidden_part, mpart, out_all, qh, kh, vh, qkv_all, hidden_res, grad_hidden, block_input
        )
        block_output, grad_input, grad_qkv_w, grad_out_w, grad_hidden_w, both = close(
            groups, rows, width // HD, held, normed_one, attn_norm_gain, down_bias, mlp_sums, unit_sums
        )
        (
            block_output, grad_input, grad_qkv_w, grad_out_w, grad_hidden_w, grad_down_w, grad_qv, grad_hidden_b, *both
        ) = deliver(
            width, units, block_output, grad_input, grad_qkv_w, grad_out_w, grad_hidden_w, grad_down_w, both
        )
        grad_qkv_w = grad_qkv_w.transpose(1, 0, 2)
        grad_out_w, grad_down_w = grad_out_w.T, grad_down_w.T
    else:
        qkv_rows = qkv_weight.reshape(-1, 3 * width)
        shift = jnp.concatenate([qv_bias[0], jnp.zeros_like(qv_bias[0]), qv_bias[1]])
        hidden_all, down_all = weight(hidden_weight), weight(down_rows)
        qkv_all, out_all = weight(qkv_rows), weight(out_rows)
        lens = jnp.sum(key_mask, axis=1)
        in_float = block_input.astype(F32)
        normed_one = gather_rows(norm_forward(in_float, attn_norm_gain, attn_norm_bias))
        grad_full = gather_rows(grad_out)
        proj = jnp.einsum("isd,df->isf", normed_one, qkv_all, preferred_element_type=F32) + shift
        proj = proj.astype(BF16)
        mixed = attend_forward(lens, proj)
        attn_part = jnp.einsum("isf,df->isd", mixed, out_all, preferred_element_type=F32).astype(BF16)
        hidden_res = in_float + scatter_rows(attn_part) + out_bias
        normed_two = gather_rows(norm_forward(hidden_res, mlp_norm_gain, mlp_norm_bias))
        pre_act = jnp.einsum("isd,df->isf", normed_two, hidden_all, preferred_element_type=F32) + hidden_bias
        value, slope = gelu_both(pre_act)
        activated = value.astype(BF16)
        grad_act = jnp.einsum("isd,df->isf", grad_full, down_all, preferred_element_type=F32)
        grad_pre = grad_act * slope
        grad_hidden_b = jnp.sum(grad_pre, axis=(0, 1))
        grad_pre_low = grad_pre.astype(BF16)
        gpart = jnp.einsum("isf,df->isd", grad_pre_low, hidden_all, preferred_element_type=F32).astype(BF16)
        mpart = jnp.einsum("isf,df->isd", activated, down_all, preferred_element_type=F32).astype(BF16)
        block_output = (hidden_res + scatter_rows(mpart) + down_bias).astype(BF16)
        grad_float = grad_out.astype(F32)
        grad_normed = scatter_rows(gpart)
        unit, inv_std = norm_stats(hidden_res)
        grad_hidden = grad_float + norm_backward(grad_normed, unit, inv_std, mlp_norm_gain)
        hidden_full = gather_rows(grad_hidden.astype(BF16))
        mlp_sums = jnp.stack(
            [jnp.sum(v, axis=(0, 1)) for v in (grad_normed * unit, grad_normed, grad_hidden, grad_float)]
        )
        grad_hidden_w = owned(jnp.einsum("isd,isf->df", normed_two, grad_pre_low, preferred_element_type=F32))
        grad_down_w = owned(jnp.einsum("isd,isf->df", grad_full, activated, preferred_element_type=F32)).T
        grad_mixed = jnp.einsum("isd,df->isf", hidden_full, out_all, preferred_element_type=F32).astype(BF16)
        grad_proj, proj_sums = attend_backward(lens, proj, grad_mixed)
        proj_sums = jnp.sum(proj_sums, axis=(0, 1))
        npart = jnp.einsum("isf,df->isd", grad_proj, qkv_all, preferred_element_type=F32).astype(BF16)
        grad_out_w = owned(jnp.einsum("isd,isf->df", hidden_full, mixed, preferred_element_type=F32)).T
        grad_qkv_w = owned(jnp.einsum("isd,isf->df", normed_one, grad_proj, preferred_element_type=F32))
        grad_normed = scatter_rows(npart)
        unit, inv_std = norm_stats(in_float)
        grad_input = grad_hidden + norm_backward(grad_normed, unit, inv_std, attn_norm_gain)
        attn_sums = jnp.stack([jnp.sum(v, axis=(0, 1)) for v in (grad_normed * unit, grad_normed)])
        both = lax.psum(jnp.concatenate([mlp_sums, attn_sums]), ("dp", "tensor"))
        proj_sums, grad_hidden_b = lax.psum((proj_sums, grad_hidden_b), "dp")
        grad_qv = jnp.stack([proj_sums[:width], proj_sums[2 * width :]])
        grad_qkv_w = grad_qkv_w.reshape(-1, 3, width)
    return (
        block_output,
        grad_input,
        both[4],
        both[5],
        grad_qkv_w,
        grad_qv,
        grad_out_w,
        both[2],
        both[0],
        both[1],
        grad_hidden_w,
        grad_hidden_b,
        grad_down_w,
        both[3],
    )


def solution(mesh):
    return jax.shard_map(
        functools.partial(shards, mesh.shape["dp"], mesh.shape["tensor"]),
        mesh=mesh,
        in_specs=(
            P("dp", "tensor", None),
            P("dp", None),
            P(),
            P(),
            P("dp", None, "tensor"),
            P(None, "tensor"),
            P("tensor", "dp"),
            P(),
            P(),
            P(),
            P("dp", "tensor"),
            P("tensor"),
            P("tensor", "dp"),
            P(),
            P("dp", "tensor", None),
        ),
        out_specs=(
            P("dp", "tensor", None),
            P("dp", "tensor", None),
            P(),
            P(),
            P("dp", None, "tensor"),
            P(None, "tensor"),
            P("tensor", "dp"),
            P(),
            P(),
            P(),
            P("dp", "tensor"),
            P("tensor"),
            P("tensor", "dp"),
            P(),
        ),
        check_vma=False,
    )
```

profile of v0, /device:TPU:0, one launch (start us, length us, event | category | flops | bytes accessed | tf_op | source)
XLA Modules:
  0.0 284.8 jit_solution(536118883836132267)
XLA Ops:
  0.6 119.8 %front.1 = (bf16[2,4,192,1152]{3,2,1,0:T(8,128)(2,1)}, bf16[4,192,1152]{2,1,0:T(8,128)(2,1)}, bf16[2,4,192,1152]{3,2,1,0:T(8,128)(2,1)}, f32[2,184,1152]{2,1,0:T...) custom-call(bf16[2,184,1152]{2,1,0:T(8,128)(2,1)} %x_hbm.1, ...), custom_call_target="tpu_custom_call" | custom-call | tf_op jit(solution)/shard_map/front/pallas_call | solution.py:657
  120.4 75.8 %turn.1 = (bf16[2,4,192,1152]{3,2,1,0:T(8,128)(2,1)}, f32[2,184,1152]{2,1,0:T(8,128)}, bf16[1152,1152]{1,0:T(8,128)(2,1)}, bf16[2,4,192,1152]{3,2,1,0:T(8,128)(2...) custom-call(bf16[2,4,192,1152]{3,2,1,0:T(8,128)(2,1)} %get-tuple-element.53.two_hbm, ...), custom_call_target="tpu_custom_call" | custom-call | tf_op jit(solution)/shard_map/turn/pallas_call | solution.py:873
  196.3 83.0 %close.1 = (bf16[2,184,1152]{2,1,0:T(8,128)(2,1)}, f32[2,184,1152]{2,1,0:T(8,128)}, f32[3,144,288]{2,1,0:T(8,128)}, f32[144,288]{1,0:T(8,128)}, f32[144,1076]{1,0:T(8,128)}, /*index=5*/f32[8,1152]{1,0:T(8,128)}) custom-call(bf16[2,4,192,1152]{3,2,1,0:T(8,128)(2,1)} %get-tuple-element.58.glow_hbm, bf16[2,4,192,384]{3,2,1,0:T(8,128)(2,1)} %get-tuple-element.59.mixed_hbm, ...), custom_call_target="tpu_custom_call" | custom-call | tf_op jit(solution)/shard_map/close/pallas_call | solution.py:1072
  279.3 5.4 %deliver.1 = (bf16[2,184,1152]{2,1,0:T(8,128)(2,1)}, f32[2,184,1152]{2,1,0:T(8,128)}, f32[3,144,288]{2,1,0:T(8,128)}, f32[144,288]{1,0:T(8,128)}, f32[144,1076]{...) custom-call(bf16[2,184,1152]{2,1,0:T(8,128)(2,1)} %get-tuple-element, ...), custom_call_target="tpu_custom_call" | custom-call | tf_op jit(solution)/shard_map/deliver/pallas_call | solution.py:1126
where the time goes:
time: 285 us
  Pallas kernels  284 us (100%)
    pallas_call x1, Pallas kernels, front(): pl.pallas_call(functools.partial(front_body, groups, rows, heads), out_sh...  120 us
    pallas_call x1, Pallas kernels, close(): pl.pallas_call(functools.partial(close_body, groups, rows, heads), out_sh...  83 us
    pallas_call x1, Pallas kernels, turn(): pl.pallas_call(functools.partial(turn_body, groups, rows), out_shape=tupl...  75.8 us

commit v1 on v0

--- a/solution.py
+++ b/solution.py
@@ -219,6 +219,16 @@
     pl.semaphore_wait(barrier, len(peers))
 
 
+def greet_all(groups):
+    row, me = lax.axis_index("dp"), lax.axis_index("tensor")
+    barrier = pltpu.get_barrier_semaphore()
+    peers = [{"dp": lax.rem(row + k, groups)} for k in range(1, groups)]
+    peers += [{"tensor": lax.rem(me + k, 4)} for k in range(1, 4)]
+    for peer in peers:
+        pl.semaphore_signal(barrier, inc=1, device_id=peer, device_id_type=MESH)
+    pl.semaphore_wait(barrier, len(peers))
+
+
 def remote(src, dst, send, recv, peer):
     return pltpu.make_async_remote_copy(
         src_ref=src,
@@ -328,7 +338,7 @@
 
 
 def params(cid):
-    return pltpu.CompilerParams(collective_id=cid, has_side_effects=True, vmem_limit_bytes=60 << 20)
+    return pltpu.CompilerParams(collective_id=cid, has_side_effects=True, vmem_limit_bytes=67043328)
 
 
 def lanes(width):
@@ -457,221 +467,6 @@
             made.wait()
 
 
-def front_body(
-    groups, rows, heads,
-    x_ref, grad_ref, mask_ref, gain_one, bias_one, bias_out, gain_two, bias_two, qv_ref, wq_ref, wo_ref, wh_ref, wd_ref,
-    one_out, full_out, two_out, hidden_out, qh_out, kh_out, vh_out, mixed_out, wq_out, wo_out, wh_out, wd_out,
-    one_ref, full_ref, two_ref, hidden_ref, qh, kh, vh, mixed_ref, wq_all, wo_all, wh_all, wd_all,
-    oh, part_ref, near, far, passing, osem,
-    asend, arecv, fsend, frecv, ssend, srecv, gsend, grecv, wsend, wrecv,
-):
-    images = x_ref.shape[0]
-    full = one_ref.shape[2]
-    seq = 4 * full
-    width = heads * HD
-    me, side, over, _ = plane()
-    mine = lax.axis_index("dp")
-    wq_all[mine, :, 3 * width :] = jnp.zeros_like(wq_all[mine, :, 3 * width :])
-    for c in range(3):
-        wq_all[mine, :, c * width : (c + 1) * width] = wq_ref[c]
-    weights = [Spread(groups, wq_all, wsend.at[0], wrecv.at[0])]
-    for k, (own, everyone) in enumerate(((wo_ref, wo_all), (wh_ref, wh_all), (wd_ref, wd_all))):
-        count = own.shape[1]
-        everyone[mine, :, count:] = jnp.zeros_like(everyone[mine, :, count:])
-        everyone[mine, :, :count] = own[...]
-        weights.append(Spread(groups, everyone, wsend.at[k + 1], wrecv.at[k + 1]))
-    wq, wo, wh, wd = weights
-    ones, sums, twos = [], [], []
-    for i in range(images):
-        clear_pads(one_ref.at[i], rows)
-        clear_pads(two_ref.at[i], rows)
-        ones.append(Gather(one_ref.at[i], rows, asend.at[i], arecv.at[i]))
-        sums.append(Scatter(part_ref.at[i], rows, near.at[i], far.at[i], passing.at[i], ssend.at[i], srecv.at[i]))
-        twos.append(Gather(two_ref.at[i], rows, gsend.at[i], grecv.at[i]))
-    mixed_ref[:, :, :, width:] = jnp.zeros_like(mixed_ref[:, :, :, width:])
-    clear_pads(full_ref, rows)
-    grads = Gather(full_ref, rows, fsend, frecv)
-    stores = Moves(osem)
-    put_weight = [stores.plan(a, b) for a, b in ((wq_all, wq_out), (wo_all, wo_out), (wh_all, wh_out), (wd_all, wd_out))]
-    put_full = stores.plan(full_ref, full_out)
-    pairs = (
-        (one_ref, one_out), (two_ref, two_out), (hidden_ref, hidden_out), (qh, qh_out), (kh, kh_out), (vh, vh_out),
-        (mixed_ref, mixed_out),
-    )
-    put = [[stores.plan(a.at[i], b.at[i]) for a, b in pairs] for i in range(images)]
-
-    def enter(i):
-        one_ref[i, me, :rows] = norm_forward(x_ref[i].astype(F32), at_row(gain_one), at_row(bias_one))
-
-    enter(0)
-    greet_both(groups, side, over)
-    ones[0].start()
-    wq.start()
-    for i in range(1, images):
-        enter(i)
-        ones[i].start()
-    wo.start()
-    wh.start()
-    wd.start()
-    full_ref[me, :rows] = grad_ref[0]
-    for i in range(images):
-        bias, tail = key_bias(mask_ref[i : i + 1], rows, full, seq)
-        for h in range(heads):
-            kh[i, h, :, HD:] = bias
-            vh[i, h, :, HD:] = jnp.zeros_like(bias)
-            qh[i, h, :, HD:] = tail
-    for step in ones:
-        step.forward()
-    grads.start()
-    wq.hop()
-    wq.forward()
-    factor = HD**-0.5 * LOG2E
-    shift_q, shift_v = qv_ref[0:1], qv_ref[1:2]
-
-    def project(i):
-        weight = wq_all[:, :, : 3 * width].reshape(-1, 3 * width)
-
-        def block(b, _):
-            at = pl.ds(pl.multiple_of(b * full, 16), full)
-            value = dot(one_ref[i, b], weight)
-            queries = (value[:, :width] + shift_q).astype(BF16)
-            keys_in = value[:, width : 2 * width].astype(BF16)
-            values = (value[:, 2 * width :] + shift_v).astype(BF16)
-            for h in range(heads):
-                here = slice(h * HD, (h + 1) * HD)
-                qh[i, h, at, :HD] = queries[:, here]
-                kh[i, h, at, :HD] = keys_in[:, here]
-                vh[i, h, at, :HD] = values[:, here]
-            return 0
-
-        lax.fori_loop(0, 4, block, 0)
-
-    def attend(i):
-        def head(h, _):
-            probs = soft_open(kh[i, h], qh[i, h], factor)
-            oh[h] = dot(vh[i, h, :, :HD].T, probs.astype(BF16)).T.astype(BF16)
-            return 0
-
-        lax.fori_loop(0, heads, head, 0, unroll=2)
-        for h in range(heads):
-            for b in range(4):
-                mixed_ref[i, b, :, h * HD : (h + 1) * HD] = oh[h, b * full : (b + 1) * full]
-
-    def combine(i):
-        weight = wo_all[:, :, :width].reshape(-1, width)
-
-        def block(b, _):
-            part_ref[i, b] = dot(mixed_ref[i, b, :, :width], weight, NT).astype(BF16)
-            return 0
-
-        lax.fori_loop(0, 4, block, 0)
-
-    def ready(k):
-        ones[k].arrive()
-        put[k][0].start()
-        if k == 0:
-            wq.arrive()
-            put_weight[0].start()
-
-    def between(k):
-        for made in put[k][3:]:
-            made.start()
-        if k == 0:
-            grads.forward()
-            wo.hop()
-            wo.forward()
-            wh.hop()
-            wo.arrive()
-            put_weight[1].start()
-
-    def send(k):
-        if k > 0:
-            sums[k - 1].forward()
-        sums[k].start()
-
-    def image(i, _):
-        for_image(i, images, ready)
-        project(i)
-        attend(i)
-        for_image(i, images, between)
-        combine(i)
-        for_image(i, images, send)
-        return 0
-
-    lax.fori_loop(0, images, image, 0)
-
-    def settle(i):
-        sums[i].arrive()
-        hidden = x_ref[i].astype(F32) + sums[i].total(pl.ds(0, rows)) + at_row(bias_out)
-        hidden_ref[i] = hidden
-        two_ref[i, me, :rows] = norm_forward(hidden, at_row(gain_two), at_row(bias_two))
-        twos[i].start()
-        put[i][2].start()
-
-    for i in range(images - 1):
-        settle(i)
-    sums[-1].forward()
-    wd.hop()
-    for i in range(images - 1):
-        twos[i].forward()
-    settle(images - 1)
-    grads.arrive()
-    put_full.start()
-    wh.forward()
-    twos[-1].forward()
-    wh.arrive()
-    put_weight[2].start()
-    wd.forward()
-    for i in range(images):
-        twos[i].arrive()
-        put[i][1].start()
-    wd.arrive()
-    put_weight[3].start()
-    for step in ones + sums + twos + weights + [grads]:
-        step.finish()
-    stores.finish()
-
-
-def front(groups, block_input, grad_out, key_mask, vectors, qv_bias, wq, wo, wh, wd):
-    images, rows, model = block_input.shape
-    full = pad_rows(rows)
-    width = wo.shape[1]
-    units = wh.shape[1]
-    heads = width // HD
-    seq = 4 * full
-    depth = wo.shape[0]
-    held = [
-        ((images, 4, full, model), BF16),
-        ((4, full, model), BF16),
-        ((images, 4, full, model), BF16),
-        ((images, rows, model), F32),
-        ((images, heads, seq, 128), BF16),
-        ((images, heads, seq, 128), BF16),
-        ((images, heads, seq, 128), BF16),
-        ((images, 4, full, lanes(width)), BF16),
-        ((groups, depth, lanes(3 * width)), BF16),
-        ((groups, depth, lanes(width)), BF16),
-        ((groups, depth, lanes(units)), BF16),
-        ((groups, depth, lanes(units)), BF16),
-    ]
-    return pl.pallas_call(
-        functools.partial(front_body, groups, rows, heads),
-        out_shape=tuple(jax.ShapeDtypeStruct(*h) for h in held),
-        in_specs=[VMEM] * 13,
-        out_specs=(ANY,) * len(held),
-        scratch_shapes=[pltpu.VMEM(*h) for h in held]
-        + [pltpu.VMEM((heads, seq, HD), BF16), pltpu.VMEM((images, 4, full, model), BF16)]
-        + scatter_scratch(images, full, model)
-        + [pltpu.SemaphoreType.DMA((7 * images + 5,))]
-        + sems(images, STEPS)
-        + sems(STEPS)
-        + sems(images, STEPS) * 2
-        + sems(4, groups),
-        compiler_params=params(0),
-        name="front",
-    )(block_input, grad_out, key_mask, *vectors, qv_bias, wq, wo, wh, wd)
-
-
 class Reduce:
     def __init__(self, groups, grad_ref, twin_ref, far_ref, tsend, trecv, fsend, frecv):
         self.grad_ref, self.twin_ref, self.far_ref = grad_ref, twin_ref, far_ref
@@ -736,57 +531,197 @@
     lax.fori_loop(0, model // tile, part, 0)
 
 
-def turn_body(
-    groups, rows,
-    two_hbm, full_hbm, wh_hbm, wd_hbm, hidden_hbm, grad_ref, gain_ref, hb_ref,
-    glow_hbm, ghid_hbm, gwh_hbm, mpart_hbm, gwd_ref, sums_ref, hsum_ref,
-    two_ref, wh_ref, wd_ref, hidden_ref, glow_ref, ghid_ref, gwh_ref, mpart_ref,
-    full_ref, act_ref, gpl_ref, gpart_ref, gwd_part, lsem, osem,
-    near, far, passing, twin, away, tsend, trecv, fsend, frecv, ssend, srecv, gsend, grecv, asend, arecv,
+def main_body(
+    groups, rows, heads,
+    x_ref, grad_ref, mask_ref, gain_one, bias_one, bias_out, gain_two, bias_two, qv_ref, hb_ref,
+    wq_ref, wo_ref, wh_ref, wd_ref,
+    one_out, hidden_out, qh_out, kh_out, vh_out, mixed_out, wq_out, wo_out, glow_out, ghid_out, gwh_out, mpart_out,
+    gwd_ref, sums_ref, hsum_ref,
+    one_ref, full_ref, two_ref, hidden_ref, qh, kh, vh, mixed_ref, wq_all, wo_all, wh_all, wd_all,
+    oh, part_ref, ghid_ref, act_ref, gpl_ref, gwh_part, gwd_part,
+    near, far, passing, osem, twin, away, tsend, trecv, fsend, frecv,
+    asend, arecv, csend, crecv, ssend, srecv, gsend, grecv, usend, urecv, vsend, vrecv, wsend, wrecv,
 ):
-    images, _, full, model = two_ref.shape
+    images = x_ref.shape[0]
+    _, _, full, model = one_ref.shape
     units = hb_ref.shape[0]
+    seq = 4 * full
+    width = heads * HD
     me, side, over, _ = plane()
-    loads, stores = Moves(lsem), Moves(osem)
-    got = [[loads.start(two_hbm.at[0], two_ref.at[0])]]
-    got[0].append(loads.start(wh_hbm, wh_ref))
-    got[0].append(loads.start(full_hbm, full_ref.at[0]))
-    got[0].append(loads.start(wd_hbm, wd_ref))
+    mine = lax.axis_index("dp")
+    wq_all[mine, :, 3 * width :] = jnp.zeros_like(wq_all[mine, :, 3 * width :])
+    for c in range(3):
+        wq_all[mine, :, c * width : (c + 1) * width] = wq_ref[c]
+    weights = [Spread(groups, wq_all, wsend.at[0], wrecv.at[0])]
+    for k, (own, everyone) in enumerate(((wo_ref, wo_all), (wh_ref, wh_all), (wd_ref, wd_all))):
+        count = own.shape[1]
+        everyone[mine, :, count:] = jnp.zeros_like(everyone[mine, :, count:])
+        everyone[mine, :, :count] = own[...]
+        weights.append(Spread(groups, everyone, wsend.at[k + 1], wrecv.at[k + 1]))
+    wq, wo, wh, wd = weights
+    ones, sums, twos, grads, turns, lows = [], [], [], [], [], []
+    for i in range(images):
+        for ref in (one_ref, two_ref, full_ref):
+            clear_pads(ref.at[i], rows)
+        slots = (near.at[i], far.at[i], passing.at[i])
+        ones.append(Gather(one_ref.at[i], rows, asend.at[i], arecv.at[i]))
+        grads.append(Gather(full_ref.at[i], rows, csend.at[i], crecv.at[i]))
+        sums.append(Scatter(part_ref.at[i], rows, *slots, ssend.at[i], srecv.at[i]))
+        twos.append(Gather(two_ref.at[i], rows, gsend.at[i], grecv.at[i]))
+        turns.append(Scatter(part_ref.at[i], rows, *slots, usend.at[i], urecv.at[i]))
+        if i < images - 1:
+            lows.append(Gather(one_ref.at[i], rows, vsend.at[i], vrecv.at[i]))
+    down = Reduce(groups, gwd_part, twin, away, tsend, trecv, fsend, frecv)
+    stores = Moves(osem)
+    put_wq, put_wo, put_gwh = [
+        stores.plan(a, b) for a, b in ((wq_all, wq_out), (wo_all, wo_out), (gwh_part, gwh_out))
+    ]
+    pairs = (
+        (one_ref, one_out), (hidden_ref, hidden_out), (qh, qh_out), (kh, kh_out), (vh, vh_out), (mixed_ref, mixed_out),
+        (two_ref, mpart_out), (ghid_ref, ghid_out),
+    )
+    put = [[stores.plan(a.at[i], b.at[i]) for a, b in pairs] for i in range(images)]
+    put_low = [stores.plan(one_ref.at[i], glow_out.at[i]) for i in range(images - 1)]
+
+    def enter(i):
+        one_ref[i, me, :rows] = norm_forward(x_ref[i].astype(F32), at_row(gain_one), at_row(bias_one))
+
+    enter(0)
+    greet_both(groups, side, over)
+    ones[0].start()
+    wq.start()
     for i in range(1, images):
-        got.append([loads.start(two_hbm.at[i], two_ref.at[i])])
-    got_hidden = loads.start(hidden_hbm, hidden_ref)
-    put_mpart = [stores.plan(mpart_ref.at[i], mpart_hbm.at[i]) for i in range(images)]
-    put_ghid = [stores.plan(ghid_ref.at[i], ghid_hbm.at[i]) for i in range(images)]
-    put_glow = [stores.plan(glow_ref.at[i], glow_hbm.at[i]) for i in range(images)]
-    put_gwh = stores.plan(gwh_ref, gwh_hbm)
+        enter(i)
+        ones[i].start()
+    for step in (wo, wh, wd):
+        step.start()
+    mixed_ref[:, :, :, width:] = jnp.zeros_like(mixed_ref[:, :, :, width:])
     hsum_ref[...] = jnp.zeros_like(hsum_ref)
-    sums, gathers, grads = [], [], [None]
     for i in range(images):
-        clear_pads(glow_ref.at[i], rows)
-        sums.append(Scatter(gpart_ref.at[i], rows, near.at[i], far.at[i], passing.at[i], ssend.at[i], srecv.at[i]))
-        gathers.append(Gather(glow_ref.at[i], rows, gsend.at[i], grecv.at[i]))
-        if i > 0:
-            clear_pads(full_ref.at[i], rows)
-            full_ref[i, me, :rows] = grad_ref[i]
-            grads.append(Gather(full_ref.at[i], rows, asend.at[i], arecv.at[i]))
-    down = Reduce(groups, gwd_part, twin, away, tsend, trecv, fsend, frecv)
-    greet_both(groups, side, over)
+        full_ref[i, me, :rows] = grad_ref[i]
+        bias, tail = key_bias(mask_ref[i : i + 1], rows, full, seq)
+        for h in range(heads):
+            kh[i, h, :, HD:] = bias
+            vh[i, h, :, HD:] = jnp.zeros_like(bias)
+            qh[i, h, :, HD:] = tail
+    for step in ones:
+        step.forward()
+    grads[0].start()
+    wq.hop()
+    wq.forward()
+    factor = HD**-0.5 * LOG2E
+    shift_q, shift_v = qv_ref[0:1], qv_ref[1:2]
+
+    def project(i):
+        weight = wq_all[:, :, : 3 * width].reshape(-1, 3 * width)
+
+        def block(b, _):
+            at = pl.ds(pl.multiple_of(b * full, 16), full)
+            value = dot(one_ref[i, b], weight)
+            queries = (value[:, :width] + shift_q).astype(BF16)
+            keys_in = value[:, width : 2 * width].astype(BF16)
+            values = (value[:, 2 * width :] + shift_v).astype(BF16)
+            for h in range(heads):
+                here = slice(h * HD, (h + 1) * HD)
+                qh[i, h, at, :HD] = queries[:, here]
+                kh[i, h, at, :HD] = keys_in[:, here]
+                vh[i, h, at, :HD] = values[:, here]
+            return 0
+
+        lax.fori_loop(0, 4, block, 0)
+
+    def attend(i):
+        def head(h, _):
+            probs = soft_open(kh[i, h], qh[i, h], factor)
+            oh[h] = dot(vh[i, h, :, :HD].T, probs.astype(BF16)).T.astype(BF16)
+            return 0
+
+        lax.fori_loop(0, heads, head, 0, unroll=2)
+        for h in range(heads):
+            for b in range(4):
+                mixed_ref[i, b, :, h * HD : (h + 1) * HD] = oh[h, b * full : (b + 1) * full]
+
+    def combine(i):
+        weight = wo_all[:, :, :width].reshape(-1, width)
+
+        def block(b, _):
+            part_ref[i, b] = dot(mixed_ref[i, b, :, :width], weight, NT).astype(BF16)
+            return 0
+
+        lax.fori_loop(0, 4, block, 0)
+
+    def ready(k):
+        ones[k].arrive()
+        put[k][0].start()
+        if k == 0:
+            wq.arrive()
+            put_wq.start()
+
+    def between(k):
+        for made in put[k][2:6]:
+            made.start()
+        if k == 0:
+            grads[0].forward()
+            wo.hop()
+            wo.forward()
+            wh.hop()
+            wo.arrive()
+            put_wo.start()
+
+    def send(k):
+        if k > 0:
+            sums[k - 1].forward()
+        sums[k].start()
+
+    def image(i, _):
+        for_image(i, images, ready)
+        project(i)
+        attend(i)
+        for_image(i, images, between)
+        combine(i)
+        for_image(i, images, send)
+        return 0
+
+    lax.fori_loop(0, images, image, 0)
+
+    def settle(i):
+        sums[i].arrive()
+        hidden = x_ref[i].astype(F32) + sums[i].total(pl.ds(0, rows)) + at_row(bias_out)
+        hidden_ref[i] = hidden
+        two_ref[i, me, :rows] = norm_forward(hidden, at_row(gain_two), at_row(bias_two))
+        twos[i].start()
+        put[i][1].start()
+
+    for i in range(images - 1):
+        settle(i)
+    sums[-1].forward()
+    wd.hop()
+    for i in range(images - 1):
+        twos[i].forward()
+    settle(images - 1)
     for step in grads[1:]:
         step.start()
+    wh.forward()
+    wd.forward()
+    twos[-1].forward()
+    for step in sums + ones:
+        step.finish()
+    for i in range(images):
+        put[i][0].wait()
     wide = lambda ref: ref[:, :, :units].reshape(model, units)
     shift = at_row(hb_ref)
 
     def ascend(i):
         def pair(c, _):
             at = pl.ds(2 * c, 2)
-            pre = dot(two_ref[i, at].reshape(2 * full, model), wide(wh_ref)) + shift
+            pre = dot(two_ref[i, at].reshape(2 * full, model), wide(wh_all)) + shift
             value, slope = gelu_both(pre)
             act_ref[i, at] = value.astype(BF16).reshape(2, full, units)
-            grad_pre = dot(full_ref[i, at].reshape(2 * full, model), wide(wd_ref)) * slope
+            grad_pre = dot(full_ref[i, at].reshape(2 * full, model), wide(wd_all)) * slope
             hsum_ref[...] += jnp.sum(grad_pre, axis=0, keepdims=True)
             low = grad_pre.astype(BF16)
             gpl_ref[i, at] = low.reshape(2, full, units)
-            gpart_ref[i, at] = dot(low, wide(wh_ref), NT).astype(BF16).reshape(2, full, model)
+            part_ref[i, at] = dot(low, wide(wh_all), NT).astype(BF16).reshape(2, full, model)
             return 0
 
         lax.fori_loop(0, 2, pair, 0)
@@ -794,95 +729,116 @@
     def descend(k, _):
         at = pl.ds(2 * lax.rem(k, 2), 2)
         i = lax.div(k, 2)
-        part = dot(act_ref[i, at].reshape(2 * full, units), wide(wd_ref), NT)
-        mpart_ref[i, at] = part.astype(BF16).reshape(2, full, model)
+        part = dot(act_ref[i, at].reshape(2 * full, units), wide(wd_all), NT)
+        two_ref[i, at] = part.astype(BF16).reshape(2, full, model)
         return 0
 
     totals = [0.0, 0.0, 0.0, 0.0]
 
-    def settle(i):
-        sums[i].arrive()
-        grad_normed = sums[i].total(pl.ds(0, rows))
+    def settle_back(i):
+        turns[i].arrive()
+        grad_normed = turns[i].total(pl.ds(0, rows))
         unit, inv_std = norm_stats(hidden_ref[i])
         upper = full_ref[i, me, :rows].astype(F32)
-        grad_hidden = upper + norm_backward(grad_normed, unit, inv_std, at_row(gain_ref))
+        grad_hidden = upper + norm_backward(grad_normed, unit, inv_std, at_row(gain_two))
         ghid_ref[i] = grad_hidden
-        glow_ref[i, me, :rows] = grad_hidden.astype(BF16)
-        gathers[i].start()
-        put_ghid[i].start()
+        put[i][7].start()
+        if i < images - 1:
+            one_ref[i, me, :rows] = grad_hidden.astype(BF16)
+            lows[i].start()
         for k, term in enumerate((grad_normed * unit, grad_normed, grad_hidden, upper)):
             totals[k] = totals[k] + jnp.sum(term, axis=0, keepdims=True)
 
-    def ready(k):
-        for made in got[k]:
-            made.wait()
-        if k > 0:
-            grads[k].arrive()
-
-    def send(k):
+    def ready_back(k):
+        twos[k].arrive()
+        if k == 0:
+            wh.arrive()
+            wd.arrive()
+        grads[k].arrive()
+
+    def send_back(k):
         if k == 0:
             for step in grads[1:]:
                 step.forward()
         if k > 0:
-            sums[k - 1].forward()
-        sums[k].start()
-
-    def image(i, _):
-        for_image(i, images, ready)
+            turns[k - 1].forward()
+        turns[k].start()
+
+    def image_back(i, _):
+        for_image(i, images, ready_back)
         ascend(i)
-        for_image(i, images, send)
+        for_image(i, images, send_back)
         return 0
 
-    lax.fori_loop(0, images, image, 0)
+    lax.fori_loop(0, images, image_back, 0)
     outer(gwd_part, full_ref, act_ref, units)
     down.start()
-    got_hidden.wait()
     for i in range(images - 1):
-        settle(i)
-    sums[-1].forward()
+        settle_back(i)
+    turns[-1].forward()
     down.pair()
-    outer(gwh_ref, two_ref, gpl_ref, units)
+    outer(gwh_part, two_ref, gpl_ref, units)
     put_gwh.start()
-    for i in range(images - 1):
-        gathers[i].forward()
-    settle(images - 1)
+    for step in lows:
+        step.forward()
+    settle_back(images - 1)
+    for step in twos:
+        step.finish()
     lax.fori_loop(0, 2 * images, descend, 0)
-    for made in put_mpart:
-        made.start()
-    gathers[-1].forward()
+    for i in range(images):
+        put[i][6].start()
     for k in range(4):
         sums_ref[k : k + 1] = totals[k]
     gwd_ref[...] = down.total()[:, :units]
+    for step, made in zip(lows, put_low):
+        step.arrive()
+        made.start()
+    for step in turns + lows + grads + weights + [down]:
+        step.finish()
     for i in range(images):
-        gathers[i].arrive()
-        put_glow[i].start()
-    for step in sums + gathers + grads[1:] + [down]:
-        step.finish()
-    stores.finish()
-
-
-def turn(groups, rows, two, full_grad, wh, wd, hidden, grad_out, gain, bias):
-    images, _, full, model = two.shape
-    units = bias.shape[0]
-    depth = model // groups
+        for made in put[i][1:]:
+            made.wait()
+    for made in put_low + [put_wq, put_wo, put_gwh]:
+        made.wait()
+
+
+def main(groups, block_input, grad_out, key_mask, vectors, qv_bias, bias, wq, wo, wh, wd):
+    images, rows, model = block_input.shape
+    full = pad_rows(rows)
+    width = wo.shape[1]
+    units = wh.shape[1]
+    heads = width // HD
+    seq = 4 * full
+    depth = wo.shape[0]
     blocks = ((images, 4, full, model), BF16)
+    own = ((images, rows, model), F32)
+    heads_wide = ((images, heads, seq, 128), BF16)
+    mixed = ((images, 4, full, lanes(width)), BF16)
     wide = ((images, 4, full, units), BF16)
-    outs = [blocks, ((images, rows, model), F32), ((model, lanes(units)), BF16), blocks]
-    ins = [blocks, (wh.shape, BF16), (wh.shape, BF16), (hidden.shape, F32)]
+    square = ((model, lanes(units)), BF16)
+    weight = lambda count: ((groups, depth, lanes(count)), BF16)
+    outs = [
+        blocks, own, heads_wide, heads_wide, heads_wide, mixed, weight(3 * width), weight(width),
+        ((images - 1, 4, full, model), BF16), own, square, blocks,
+    ]
     more = [((depth, units), F32), ((4, model), F32), ((1, units), F32)]
+    held = [blocks, blocks, blocks, own, heads_wide, heads_wide, heads_wide, mixed]
+    held += [weight(3 * width), weight(width), weight(units), weight(units)]
+    held += [((heads, seq, HD), BF16), blocks, own, wide, wide, square, square]
     return pl.pallas_call(
-        functools.partial(turn_body, groups, rows),
+        functools.partial(main_body, groups, rows, heads),
         out_shape=tuple(jax.ShapeDtypeStruct(*h) for h in outs + more),
-        in_specs=[ANY] * 5 + [VMEM] * 3,
-        out_specs=(ANY,) * 4 + (VMEM,) * 3,
-        scratch_shapes=[pltpu.VMEM(*h) for h in ins + outs + [blocks, wide, wide, blocks, ((model, lanes(units)), BF16)]]
-        + [pltpu.SemaphoreType.DMA((images + 4,)), pltpu.SemaphoreType.DMA((3 * images + 1,))]
+        in_specs=[VMEM] * 14,
+        out_specs=(ANY,) * len(outs) + (VMEM,) * len(more),
+        scratch_shapes=[pltpu.VMEM(*h) for h in held]
         + scatter_scratch(images, full, model)
+        + [pltpu.SemaphoreType.DMA((9 * images + 3,))]
         + reduce_scratch(groups, depth, units)
-        + sems(images, STEPS) * 3,
-        compiler_params=params(1),
-        name="turn",
-    )(two, full_grad, wh, wd, hidden, grad_out, gain, bias)
+        + sems(images, STEPS) * 6
+        + sems(4, groups),
+        compiler_params=params(0),
+        name="main",
+    )(block_input, grad_out, key_mask, *vectors, qv_bias, bias, wq, wo, wh, wd)
 
 
 def close_body(
@@ -896,7 +852,7 @@
     htwin, haway, htsend, htrecv, hfsend, hfrecv,
     otwin, oaway, otsend, otrecv, ofsend, ofrecv,
     qtwin, qaway, qtsend, qtrecv, qfsend, qfrecv,
-    mid, msend, mrecv, ssend, srecv, vsend, vrecv, twin_in, far_in, side_in, over_in,
+    mid, msend, mrecv, ssend, srecv, lsend, lrecv, vsend, vrecv, row_in, flat_in,
 ):
     images, _, full, model = tok.shape
     width = heads * HD
@@ -905,9 +861,10 @@
     mine = lax.axis_index("dp")
     loads = Moves(lsem)
     held = (
-        (glow_hbm, tok), (mixed_hbm, mixed_ref), (gwh_hbm, gwh_part), (mpart_hbm, mpart_ref), (wo_hbm, wo_ref),
-        (qh_hbm, qh), (kh_hbm, kh), (vh_hbm, vh), (wq_hbm, wq_ref), (hidden_hbm, hidden_ref), (ghid_hbm, ghid_ref),
-        (x_hbm, x_ref),
+        (ghid_hbm.at[images - 1], ghid_ref.at[images - 1]), (glow_hbm, tok.at[pl.ds(0, images - 1)]), (wo_hbm, wo_ref),
+        (gwh_hbm, gwh_part), (mpart_hbm, mpart_ref), (qh_hbm, qh), (kh_hbm, kh), (vh_hbm, vh), (mixed_hbm, mixed_ref),
+        (wq_hbm, wq_ref), (hidden_hbm, hidden_ref), (x_hbm, x_ref),
+        (ghid_hbm.at[pl.ds(0, images - 1)], ghid_ref.at[pl.ds(0, images - 1)]),
     )
     got = [loads.start(src, dst) for src, dst in held]
     got_one = loads.plan(one_hbm, tok)
@@ -919,27 +876,28 @@
     red_h = Reduce(groups, gwh_part, htwin, haway, htsend, htrecv, hfsend, hfrecv)
     red_o = Reduce(groups, gwo_part, otwin, oaway, otsend, otrecv, ofsend, ofrecv)
     red_q = Reduce(groups, gwq_part, qtwin, qaway, qtsend, qtrecv, qfsend, qfrecv)
-    greet_both(groups, side, over)
-    for made in got[:4]:
+    last = images - 1
+    clear_pads(tok.at[last], rows)
+    low = Gather(tok.at[last], rows, lsend, lrecv)
+    got[0].wait()
+    tok[last, me, :rows] = ghid_ref[last].astype(BF16)
+    greet_all(groups)
+    low.start()
+    for made in got[1:5]:
         made.wait()
     red_h.start()
-    for step in outs:
+    for step in outs[:-1]:
         step.start()
-    outer(gwo_part, tok, mixed_ref, width)
-    red_o.start()
-    got[4].wait()
-
-    def mix(i, _):
+
+    def mix(i):
         value = dot(tok[i].reshape(seq, model), wo_ref[:, :, :width].reshape(model, width)).astype(BF16)
         for h in range(heads):
             gh[i, h] = value[:, h * HD : (h + 1) * HD]
-        return 0
-
-    lax.fori_loop(0, images, mix, 0)
-    got_one.start()
+
+    for i in range(last):
+        mix(i)
+    low.forward()
     red_h.pair()
-    outs[0].forward()
-    red_o.pair()
     for made in got[5:]:
         made.wait()
     scale = HD**-0.5
@@ -979,13 +937,20 @@
 
     def between(k):
         if k == 0:
-            for step in outs[1:]:
+            for step in outs[:-1]:
                 step.forward()
 
     def send(k):
         if k > 0:
             sums[k - 1].forward()
         sums[k].start()
+        if k == images - 2:
+            low.arrive()
+            mix(last)
+            outer(gwo_part, tok, mixed_ref, width)
+            red_o.start()
+            low.finish()
+            got_one.start()
 
     def image(i, _):
         attend(i)
@@ -995,6 +960,7 @@
         return 0
 
     lax.fori_loop(0, images, image, 0)
+    red_o.pair()
     got_one.wait()
     outer(gwq_part, tok, gproj, 3 * width)
     red_q.start()
@@ -1012,48 +978,49 @@
         settle(i)
     red_q.pair()
     sums[-1].forward()
-    for i in range(images):
+    outs[-1].start()
+
+    def finish_out(i):
         outs[i].arrive()
         out_ref[i] = (hidden_ref[i] + outs[i].total(pl.ds(0, rows)) + at_row(bias_ref)).astype(BF16)
+
+    for i in range(images - 1):
+        finish_out(i)
     gwh_ref[...] = red_h.total()[:, : gwh_ref.shape[1]]
     gwo_ref[...] = red_o.total()[:, :width]
-    settle(images - 1)
-
     mid[0] = jnp.zeros_like(mid[0])
     mid[0, 0:4] = tsum_ref[...]
-    for k in range(2):
-        mid[0, 4 + k : 5 + k] = totals[k]
     for h in range(heads):
         for c in range(3):
             mid[0, 6:7, c * width + h * HD : c * width + (h + 1) * HD] = bsum[h, c : c + 1]
     mid[0, 7:8, : hsum_ref.shape[1]] = hsum_ref[...]
-    half = groups // 2
-    place = lax.div(mine, 2)
-    twin = over_dp(mid.at[0], twin_in, vsend.at[0], vrecv.at[0], mine + 1 - 2 * lax.rem(mine, 2))
-    twin.start()
-    twin.wait()
-    mid[1] = mid[0] + twin_in[...]
-    far_in[place] = mid[1]
+    settle(images - 1)
+
+    for k in range(2):
+        mid[0, 4 + k : 5 + k] = totals[k]
+    row_in[mine] = mid[0]
     aways = []
-    for k in range(1, half):
-        peer = lax.rem(mine + 2 * k, groups)
-        aways.append(over_dp(mid.at[1], far_in.at[place], vsend.at[k], vrecv.at[k], peer))
+    for k in range(1, groups):
+        aways.append(over_dp(mid.at[0], row_in.at[mine], vsend.at[k], vrecv.at[k], lax.rem(mine + k, groups)))
         aways[-1].start()
+    outs[-1].forward()
     for made in aways:
         made.wait()
-    held = far_in[0]
-    for k in range(1, half):
-        held = held + far_in[k]
-    mid[2] = held
-    near_sum = remote(mid.at[2], side_in, vsend.at[half], vrecv.at[half], side)
-    near_sum.start()
-    near_sum.wait()
-    mid[3] = mid[2] + side_in[...]
-    over_sum = remote(mid.at[3], over_in, vsend.at[half + 1], vrecv.at[half + 1], over)
-    over_sum.start()
-    over_sum.wait()
-    both_ref[0:6] = mid[3, 0:6] + over_in[0:6]
-    both_ref[6:8] = mid[2, 6:8]
+    held = row_in[0]
+    for k in range(1, groups):
+        held = held + row_in[k]
+    mid[1] = held
+    flat_in[me] = mid[1]
+    planes = []
+    for k in range(1, 4):
+        at = groups + k
+        planes.append(remote(mid.at[1], flat_in.at[me], vsend.at[at], vrecv.at[at], lax.rem(me + k, 4)))
+        planes[-1].start()
+    for made in planes:
+        made.wait()
+    both_ref[0:6] = (flat_in[0] + flat_in[1] + flat_in[2] + flat_in[3])[0:6]
+    both_ref[6:8] = mid[1, 6:8]
+    finish_out(images - 1)
     total = red_q.total()
     for c in range(3):
         gwq_ref[c] = total[:, c * width : (c + 1) * width]
@@ -1062,13 +1029,12 @@
 
 
 def close(groups, rows, heads, held, one, gain, bias, tsum, hsum):
-    images, _, full, model = held[0].shape
+    images, _, full, model = one.shape
     width = heads * HD
     units = hsum.shape[1]
     depth = model // groups
     seq = 4 * full
     piece = pltpu.VMEM((heads, seq, HD), BF16)
-    small = pltpu.VMEM((8, model), F32)
     return pl.pallas_call(
         functools.partial(close_body, groups, rows, heads),
         out_shape=(
@@ -1081,7 +1047,7 @@
         ),
         in_specs=[ANY] * 13 + [VMEM] * 4,
         out_specs=(VMEM,) * 6,
-        scratch_shapes=[pltpu.VMEM(h.shape, h.dtype) for h in held]
+        scratch_shapes=[pltpu.VMEM(h.shape, h.dtype) for h in (one,) + held[1:]]
         + [piece] * 3
         + [
             pltpu.VMEM((images, heads, seq, HD), BF16),
@@ -1090,16 +1056,17 @@
             pltpu.VMEM((images, 4, full, model), BF16),
             pltpu.VMEM((model, lanes(3 * width)), BF16),
             pltpu.VMEM((model, lanes(width)), BF16),
-            pltpu.SemaphoreType.DMA((13,)),
+            pltpu.SemaphoreType.DMA((14,)),
         ]
         + scatter_scratch(images, full, model) * 2
         + reduce_scratch(groups, depth, units)
         + reduce_scratch(groups, depth, width)
         + reduce_scratch(groups, depth, 3 * width)
-        + [pltpu.VMEM((4, 8, model), F32)]
+        + [pltpu.VMEM((2, 8, model), F32)]
         + sems(images, STEPS) * 2
-        + sems(groups // 2 + 2)
-        + [small, pltpu.VMEM((groups // 2, 8, model), F32), small, small],
+        + sems(STEPS)
+        + sems(groups + 4)
+        + [pltpu.VMEM((groups, 8, model), F32), pltpu.VMEM((4, 8, model), F32)],
         compiler_params=params(2),
         name="close",
     )(*held, one, gain, bias, tsum, hsum)
@@ -1176,21 +1143,20 @@
     out_rows, down_rows = out_weight.T, down_weight.T
     if flat:
         (
-            normed_one, grad_full, normed_two, hidden_res, qh, kh, vh, mixed, qkv_all, out_all, hidden_all, down_all
-        ) = front(
+            normed_one, hidden_res, qh, kh, vh, mixed, qkv_all, out_all, hidden_full, grad_hidden, hidden_part, mpart,
+            grad_down_w, mlp_sums, unit_sums,
+        ) = main(
             groups,
             block_input,
             grad_out,
             key_mask,
             (attn_norm_gain, attn_norm_bias, out_bias, mlp_norm_gain, mlp_norm_bias),
             qv_bias,
+            hidden_bias,
             qkv_weight.transpose(1, 0, 2),
             out_rows,
             hidden_weight,
             down_rows,
-        )
-        hidden_full, grad_hidden, hidden_part, mpart, grad_down_w, mlp_sums, unit_sums = turn(
-            groups, rows, normed_two, grad_full, hidden_all, down_all, hidden_res, grad_out, mlp_norm_gain, hidden_bias
         )
         held = (
             hidden_full, mixed, hidden_part, mpart, out_all, qh, kh, vh, qkv_all, hidden_res, grad_hidden, block_input

time: 285 us -> 278 us (0.975)
  Pallas kernels: 284 us -> 277 us
    pallas_call x2 -> x1, Pallas kernels: 196 us -> 181 us  [main(): pl.pallas_call(functools.partial(main_body, groups, rows, heads), out_sha...]
    pallas_call x1, Pallas kernels: 83 us -> 90.8 us  [close(): pl.pallas_call(functools.partial(close_body, groups, rows, heads), out_sh...]
where the time goes in v1:
time: 278 us
  Pallas kernels  277 us (100%)
    pallas_call x1, Pallas kernels, main(): pl.pallas_call(functools.partial(main_body, groups, rows, heads), out_sha...  181 us
    pallas_call x1, Pallas kernels, close(): pl.pallas_call(functools.partial(close_body, groups, rows, heads), out_sh...  90.8 us

profile of v1, /device:TPU:0, one launch (start us, length us, event | category | flops | bytes accessed | tf_op | source)
XLA Modules:
  0.0 277.8 jit_solution(13649288568412329142)
XLA Ops:
  0.6 180.7 %main.1 = (bf16[2,4,192,1152]{3,2,1,0:T(8,128)(2,1)}, f32[2,184,1152]{2,1,0:T(8,128)}, bf16[2,4,768,128]{3,2,1,0:T(8,128)(2,1)}, bf16[2,4,768,128]{3,2,1,0:T(8,1...) custom-call(bf16[2,184,1152]{2,1,0:T(8,128)(2,1)} %x_hbm.1, ...), custom_call_target="tpu_custom_call" | custom-call | tf_op jit(solution)/shard_map/main/pallas_call | solution.py:828
  181.4 90.8 %close.1 = (bf16[2,184,1152]{2,1,0:T(8,128)(2,1)}, f32[2,184,1152]{2,1,0:T(8,128)}, f32[3,144,288]{2,1,0:T(8,128)}, f32[144,288]{1,0:T(8,128)}, f32[144,1076]{1,0:T(8,128)}, /*index=5*/f32[8,1152]{1,0:T(8,128)}) custom-call(bf16[1,4,192,1152]{3,2,1,0:T(8,128)(2,1)} %get-tuple-element.49.glow_hbm, bf16[2,4,192,384]{3,2,1,0:T(8,128)(2,1)} %get-tuple-element.50.mixed_hbm, ...), custom_call_target="tpu_custom_call" | custom-call | tf_op jit(solution)/shard_map/close/pallas_call | solution.py:1038
  272.2 5.4 %deliver.1 = (bf16[2,184,1152]{2,1,0:T(8,128)(2,1)}, f32[2,184,1152]{2,1,0:T(8,128)}, f32[3,144,288]{2,1,0:T(8,128)}, f32[144,288]{1,0:T(8,128)}, f32[144,1076]{...) custom-call(bf16[2,184,1152]{2,1,0:T(8,128)(2,1)} %get-tuple-element, ...), custom_call_target="tpu_custom_call" | custom-call | tf_op jit(solution)/shard_map/deliver/pallas_call | solution.py:1093

commit v2 on v1

--- a/solution.py
+++ b/solution.py
@@ -209,16 +209,6 @@
     pl.semaphore_wait(barrier, len(peers))
 
 
-def greet_both(groups, side, over):
-    row = lax.axis_index("dp")
-    barrier = pltpu.get_barrier_semaphore()
-    peers = [{"tensor": side}, {"tensor": over}, {"dp": row + 1 - 2 * lax.rem(row, 2)}]
-    peers += [{"dp": lax.rem(row + 2 * k, groups)} for k in range(1, groups // 2)]
-    for peer in peers:
-        pl.semaphore_signal(barrier, inc=1, device_id=peer, device_id_type=MESH)
-    pl.semaphore_wait(barrier, len(peers))
-
-
 def greet_all(groups):
     row, me = lax.axis_index("dp"), lax.axis_index("tensor")
     barrier = pltpu.get_barrier_semaphore()
@@ -281,17 +271,18 @@
 
 
 class Scatter:
-    def __init__(self, part_ref, rows, near_ref, far_ref, pass_ref, send, recv):
+    def __init__(self, part_ref, rows, slots, send, recv):
         self.me, self.side, self.over, cross = plane()
-        self.part_ref, self.near_ref, self.far_ref, self.pass_ref = part_ref, near_ref, far_ref, pass_ref
+        self.part_ref = part_ref
+        self.own, self.other, self.far, self.passing = slots
         self.halves = low, high = halves_of(rows)
         plan = (
-            (part_ref.at[cross, low], near_ref.at[1, low], self.side),
-            (part_ref.at[cross, high], near_ref.at[1, high], self.over),
-            (part_ref.at[self.side, low], near_ref.at[0, low], self.side),
-            (part_ref.at[self.over, high], near_ref.at[0, high], self.over),
-            (pass_ref.at[low], far_ref.at[low], self.over),
-            (pass_ref.at[high], far_ref.at[high], self.side),
+            (part_ref.at[cross, low], self.other.at[low], self.side),
+            (part_ref.at[cross, high], self.other.at[high], self.over),
+            (part_ref.at[self.side, low], self.own.at[low], self.side),
+            (part_ref.at[self.over, high], self.own.at[high], self.over),
+            (self.passing.at[low], self.far.at[low], self.over),
+            (self.passing.at[high], self.far.at[high], self.side),
         )
         self.copies = [remote(src, dst, send.at[k], recv.at[k], peer) for k, (src, dst, peer) in enumerate(plan)]
 
@@ -303,7 +294,7 @@
         for k, (part, block) in enumerate(zip(self.halves, (self.over, self.side))):
             self.copies[k].wait_recv()
             mine = self.part_ref[block, part].astype(F32)
-            self.pass_ref[part] = (mine + self.near_ref[1, part].astype(F32)).astype(BF16)
+            self.passing[part] = (mine + self.other[part].astype(F32)).astype(BF16)
             self.copies[4 + k].start()
 
     def arrive(self):
@@ -312,9 +303,7 @@
 
     def total(self, rows):
         return (
-            self.part_ref[self.me, rows].astype(F32)
-            + self.near_ref[0, rows].astype(F32)
-            + self.far_ref[rows].astype(F32)
+            self.part_ref[self.me, rows].astype(F32) + self.own[rows].astype(F32) + self.far[rows].astype(F32)
         )
 
     def finish(self):
@@ -327,14 +316,6 @@
 
 def sems(*shape):
     return [pltpu.SemaphoreType.DMA(shape), pltpu.SemaphoreType.DMA(shape)]
-
-
-def scatter_scratch(images, rows, width):
-    return [
-        pltpu.VMEM((images, 2, rows, width), BF16),
-        pltpu.VMEM((images, rows, width), BF16),
-        pltpu.VMEM((images, rows, width), BF16),
-    ]
 
 
 def params(cid):
@@ -384,6 +365,13 @@
     return grown * (1.0 / total)
 
 
+def block_of(ref, block, groups):
+    if len(ref.shape) == 3:
+        return ref.at[block]
+    depth = ref.shape[0] // groups
+    return ref.at[pl.ds(pl.multiple_of(block * depth, 16), depth)]
+
+
 def over_dp(src, dst, send, recv, peer):
     return pltpu.make_async_remote_copy(
         src_ref=src, dst_ref=dst, send_sem=send, recv_sem=recv, device_id={"dp": peer}, device_id_type=MESH
@@ -399,17 +387,17 @@
         self.relayed = half == 4
         self.out, self.back = [], []
         for k in range(half):
-            came = all_ref.at[lax.rem(row + groups - 2 * k, groups)]
+            came = block_of(all_ref, lax.rem(row + groups - 2 * k, groups), groups)
             self.back.append(over_dp(came, came, send.at[half + k], recv.at[half + k], twin))
             if k > 0:
-                mine = all_ref.at[row]
+                mine = block_of(all_ref, row, groups)
                 self.out.append(over_dp(mine, mine, send.at[k], recv.at[k], lax.rem(row + 2 * k, groups)))
         self.asked = {}
         if self.relayed:
             self.asked = {0: chip != 3, 2: chip != 0}
             self.inner = (chip == 1) | (chip == 2)
             up = lax.div(chip, 2)
-            came = all_ref.at[lax.rem(row + 4, groups)]
+            came = block_of(all_ref, lax.rem(row + 4, groups), groups)
             self.relay = over_dp(came, came, send.at[0], recv.at[1 + 2 * up], row + 4 * up - 2)
 
     def where(self, k, act):
@@ -469,21 +457,29 @@
 
 class Reduce:
     def __init__(self, groups, grad_ref, twin_ref, far_ref, tsend, trecv, fsend, frecv):
-        self.grad_ref, self.twin_ref, self.far_ref = grad_ref, twin_ref, far_ref
+        self.grad_ref = grad_ref
         depth = grad_ref.shape[0] // groups
+        if far_ref is None:
+            near, first = twin_ref, depth * (groups // 2)
+            self.twin = lambda slot: near.at[pl.ds(pl.multiple_of(slot * depth, 16), depth)]
+            self.far = [near.at[pl.ds(first + k * depth, depth)] for k in range(groups // 2 - 1)]
+        else:
+            self.twin = lambda slot: twin_ref.at[slot]
+            self.far = [far_ref.at[k] for k in range(groups // 2 - 1)]
         rows = lambda block: pl.ds(pl.multiple_of(block * depth, 16), depth)
         row = lax.axis_index("dp")
         core = lax.rem(row, 2)
-        self.slot, self.mine = lax.div(row, 2), rows(row)
+        self.kept, self.mine = self.twin(lax.div(row, 2)), rows(row)
         self.near, self.away = [], []
         for k in range(groups // 2):
             theirs = grad_ref.at[rows(2 * k + 1 - core)]
-            self.near.append(over_dp(theirs, twin_ref.at[k], tsend.at[k], trecv.at[k], row + 1 - 2 * core))
+            self.near.append(over_dp(theirs, self.twin(k), tsend.at[k], trecv.at[k], row + 1 - 2 * core))
         for k in range(1, groups // 2):
             peer = lax.rem(row + 2 * k, groups)
             slot = lax.div(peer, 2)
-            made = over_dp(twin_ref.at[slot], far_ref.at[k - 1], fsend.at[k], frecv.at[k], peer)
-            self.away.append((slot, rows(peer), made))
+            held = self.twin(slot)
+            made = over_dp(held, self.far[k - 1], fsend.at[k], frecv.at[k], peer)
+            self.away.append((held, rows(peer), made))
 
     def start(self):
         for made in self.near:
@@ -492,16 +488,15 @@
     def pair(self):
         for made in self.near:
             made.wait_recv()
-        for slot, part, made in self.away:
-            mine = self.grad_ref[part].astype(F32)
-            self.twin_ref[slot] = (self.twin_ref[slot].astype(F32) + mine).astype(BF16)
+        for held, part, made in self.away:
+            held[...] = (held[...].astype(F32) + self.grad_ref[part].astype(F32)).astype(BF16)
             made.start()
 
     def total(self):
-        value = self.twin_ref[self.slot].astype(F32) + self.grad_ref[self.mine].astype(F32)
-        for k, (_, _, made) in enumerate(self.away):
+        value = self.kept[...].astype(F32) + self.grad_ref[self.mine].astype(F32)
+        for (_, _, made), came in zip(self.away, self.far):
             made.wait_recv()
-            value = value + self.far_ref[k].astype(F32)
+            value = value + came[...].astype(F32)
         return value
 
     def finish(self):
@@ -518,8 +513,9 @@
     images, blocks, full, model = left_ref.shape
     count = images * blocks * full
     tile = 384
-    if out_ref.shape[1] > width:
-        out_ref[:, width:] = jnp.zeros_like(out_ref[:, width:])
+    extra = out_ref.shape[1] - width
+    if extra > 0:
+        out_ref[:, width:] = jnp.zeros((out_ref.shape[0], extra), BF16)
 
     def part(c, _):
         at = pl.ds(pl.multiple_of(c * tile, tile), tile)
@@ -531,22 +527,25 @@
     lax.fori_loop(0, model // tile, part, 0)
 
 
-def main_body(
+def whole_body(
     groups, rows, heads,
-    x_ref, grad_ref, mask_ref, gain_one, bias_one, bias_out, gain_two, bias_two, qv_ref, hb_ref,
+    x_ref, grad_ref, mask_ref, gain_one, bias_one, bias_out, gain_two, bias_two, bias_down, qv_ref, hb_ref,
     wq_ref, wo_ref, wh_ref, wd_ref,
-    one_out, hidden_out, qh_out, kh_out, vh_out, mixed_out, wq_out, wo_out, glow_out, ghid_out, gwh_out, mpart_out,
-    gwd_ref, sums_ref, hsum_ref,
+    one_out, block_out, gin_out, gwq_ref, gwo_ref, gwh_ref, gwd_ref, both_ref,
     one_ref, full_ref, two_ref, hidden_ref, qh, kh, vh, mixed_ref, wq_all, wo_all, wh_all, wd_all,
-    oh, part_ref, ghid_ref, act_ref, gpl_ref, gwh_part, gwd_part,
-    near, far, passing, osem, twin, away, tsend, trecv, fsend, frecv,
-    asend, arecv, csend, crecv, ssend, srecv, gsend, grecv, usend, urecv, vsend, vrecv, wsend, wrecv,
+    gq, part_ref, ghid_ref, act_ref, gpl_ref, gwh_part, gwd_part, gwo_part, slots, osem,
+    dtwin, daway, dtsend, dtrecv, dfsend, dfrecv,
+    otwin, oaway, otsend, otrecv, ofsend, ofrecv,
+    htsend, htrecv, hfsend, hfrecv, qtsend, qtrecv, qfsend, qfrecv,
+    gsend, grecv, wsend, wrecv,
+    hsum, bsum, mid, row_in, flat_in, vsend, vrecv,
 ):
     images = x_ref.shape[0]
     _, _, full, model = one_ref.shape
     units = hb_ref.shape[0]
     seq = 4 * full
     width = heads * HD
+    last = images - 1
     me, side, over, _ = plane()
     mine = lax.axis_index("dp")
     wq_all[mine, :, 3 * width :] = jnp.zeros_like(wq_all[mine, :, 3 * width :])
@@ -555,39 +554,47 @@
     weights = [Spread(groups, wq_all, wsend.at[0], wrecv.at[0])]
     for k, (own, everyone) in enumerate(((wo_ref, wo_all), (wh_ref, wh_all), (wd_ref, wd_all))):
         count = own.shape[1]
-        everyone[mine, :, count:] = jnp.zeros_like(everyone[mine, :, count:])
-        everyone[mine, :, :count] = own[...]
+        place = block_of(everyone, mine, groups)
+        place[:, count:] = jnp.zeros((own.shape[0], everyone.shape[-1] - count), BF16)
+        place[:, :count] = own[...]
         weights.append(Spread(groups, everyone, wsend.at[k + 1], wrecv.at[k + 1]))
     wq, wo, wh, wd = weights
-    ones, sums, twos, grads, turns, lows = [], [], [], [], [], []
+    ones, sums, twos, grads, turns, lows, outs, backs = [], [], [], [], [], [], [], []
     for i in range(images):
         for ref in (one_ref, two_ref, full_ref):
             clear_pads(ref.at[i], rows)
-        slots = (near.at[i], far.at[i], passing.at[i])
-        ones.append(Gather(one_ref.at[i], rows, asend.at[i], arecv.at[i]))
-        grads.append(Gather(full_ref.at[i], rows, csend.at[i], crecv.at[i]))
-        sums.append(Scatter(part_ref.at[i], rows, *slots, ssend.at[i], srecv.at[i]))
-        twos.append(Gather(two_ref.at[i], rows, gsend.at[i], grecv.at[i]))
-        turns.append(Scatter(part_ref.at[i], rows, *slots, usend.at[i], urecv.at[i]))
-        if i < images - 1:
-            lows.append(Gather(one_ref.at[i], rows, vsend.at[i], vrecv.at[i]))
-    down = Reduce(groups, gwd_part, twin, away, tsend, trecv, fsend, frecv)
-    stores = Moves(osem)
-    put_wq, put_wo, put_gwh = [
-        stores.plan(a, b) for a, b in ((wq_all, wq_out), (wo_all, wo_out), (gwh_part, gwh_out))
-    ]
-    pairs = (
-        (one_ref, one_out), (hidden_ref, hidden_out), (qh, qh_out), (kh, kh_out), (vh, vh_out), (mixed_ref, mixed_out),
-        (two_ref, mpart_out), (ghid_ref, ghid_out),
-    )
-    put = [[stores.plan(a.at[i], b.at[i]) for a, b in pairs] for i in range(images)]
-    put_low = [stores.plan(one_ref.at[i], glow_out.at[i]) for i in range(images - 1)]
+        pair = lambda k: (gsend.at[k, i], grecv.at[k, i])
+        four = [slots.at[i, k] for k in range(4)]
+        spare = [act_ref.at[i, k] for k in range(4)]
+        ones.append(Gather(one_ref.at[i], rows, *pair(0)))
+        grads.append(Gather(full_ref.at[i], rows, *pair(1)))
+        sums.append(Scatter(part_ref.at[i], rows, four, *pair(2)))
+        twos.append(Gather(two_ref.at[i], rows, *pair(3)))
+        turns.append(Scatter(part_ref.at[i], rows, four, *pair(4)))
+        lows.append(Gather(one_ref.at[i], rows, *pair(5)))
+        outs.append(Scatter(two_ref.at[i], rows, spare, *pair(6)))
+        backs.append(Scatter(part_ref.at[i], rows, four, *pair(7)))
+    down = Reduce(groups, gwd_part, dtwin, daway, dtsend, dtrecv, dfsend, dfrecv)
+    red_h = Reduce(groups, gwh_part, wh_all.at[:, pl.ds(0, lanes(units))], None, htsend, htrecv, hfsend, hfrecv)
+    red_o = Reduce(groups, gwo_part, otwin, oaway, otsend, otrecv, ofsend, ofrecv)
+    gwq_part = gwd_part.at[:, pl.ds(0, lanes(3 * width))]
+    red_q = Reduce(groups, gwq_part, wd_all.at[:, pl.ds(0, lanes(3 * width))], None, qtsend, qtrecv, qfsend, qfrecv)
+    moves = Moves(osem)
+    keep_one = [moves.plan(one_ref.at[i], one_out.at[i]) for i in range(images)]
+    take_one = [moves.plan(one_out.at[i], full_ref.at[i]) for i in range(images)]
+    take_grad = [moves.plan(grad_ref.at[i], full_ref.at[i, me, pl.ds(0, rows)]) for i in range(images)]
+    for made in take_grad:
+        made.start()
+    put_out = [moves.plan(two_ref.at[i, me, pl.ds(0, rows)], block_out.at[i]) for i in range(images)]
+    put_gin = [moves.plan(ghid_ref.at[i], gin_out.at[i]) for i in range(images)]
 
     def enter(i):
         one_ref[i, me, :rows] = norm_forward(x_ref[i].astype(F32), at_row(gain_one), at_row(bias_one))
 
     enter(0)
-    greet_both(groups, side, over)
+    for made in take_grad:
+        made.wait()
+    greet_all(groups)
     ones[0].start()
     wq.start()
     for i in range(1, images):
@@ -595,10 +602,10 @@
         ones[i].start()
     for step in (wo, wh, wd):
         step.start()
+    hsum[...] = jnp.zeros_like(hsum)
+    bsum[...] = jnp.zeros_like(bsum)
     mixed_ref[:, :, :, width:] = jnp.zeros_like(mixed_ref[:, :, :, width:])
-    hsum_ref[...] = jnp.zeros_like(hsum_ref)
     for i in range(images):
-        full_ref[i, me, :rows] = grad_ref[i]
         bias, tail = key_bias(mask_ref[i : i + 1], rows, full, seq)
         for h in range(heads):
             kh[i, h, :, HD:] = bias
@@ -609,7 +616,7 @@
     grads[0].start()
     wq.hop()
     wq.forward()
-    factor = HD**-0.5 * LOG2E
+    scale = HD**-0.5
     shift_q, shift_v = qv_ref[0:1], qv_ref[1:2]
 
     def project(i):
@@ -632,14 +639,14 @@
 
     def attend(i):
         def head(h, _):
-            probs = soft_open(kh[i, h], qh[i, h], factor)
-            oh[h] = dot(vh[i, h, :, :HD].T, probs.astype(BF16)).T.astype(BF16)
+            probs = soft_open(kh[i, h], qh[i, h], scale * LOG2E)
+            gq[h] = dot(vh[i, h, :, :HD].T, probs.astype(BF16)).T.astype(BF16)
             return 0
 
         lax.fori_loop(0, heads, head, 0, unroll=2)
         for h in range(heads):
             for b in range(4):
-                mixed_ref[i, b, :, h * HD : (h + 1) * HD] = oh[h, b * full : (b + 1) * full]
+                mixed_ref[i, b, :, h * HD : (h + 1) * HD] = gq[h, b * full : (b + 1) * full]
 
     def combine(i):
         weight = wo_all[:, :, :width].reshape(-1, width)
@@ -652,21 +659,17 @@
 
     def ready(k):
         ones[k].arrive()
-        put[k][0].start()
+        keep_one[k].start()
         if k == 0:
             wq.arrive()
-            put_wq.start()
 
     def between(k):
-        for made in put[k][2:6]:
-            made.start()
         if k == 0:
             grads[0].forward()
             wo.hop()
             wo.forward()
             wh.hop()
             wo.arrive()
-            put_wo.start()
 
     def send(k):
         if k > 0:
@@ -690,15 +693,14 @@
         hidden_ref[i] = hidden
         two_ref[i, me, :rows] = norm_forward(hidden, at_row(gain_two), at_row(bias_two))
         twos[i].start()
-        put[i][1].start()
-
-    for i in range(images - 1):
+
+    for i in range(last):
         settle(i)
     sums[-1].forward()
     wd.hop()
-    for i in range(images - 1):
+    for i in range(last):
         twos[i].forward()
-    settle(images - 1)
+    settle(last)
     for step in grads[1:]:
         step.start()
     wh.forward()
@@ -706,9 +708,9 @@
     twos[-1].forward()
     for step in sums + ones:
         step.finish()
-    for i in range(images):
-        put[i][0].wait()
-    wide = lambda ref: ref[:, :, :units].reshape(model, units)
+    for made in keep_one:
+        made.wait()
+    wide = lambda ref: ref[:, :units]
     shift = at_row(hb_ref)
 
     def ascend(i):
@@ -716,11 +718,11 @@
             at = pl.ds(2 * c, 2)
             pre = dot(two_ref[i, at].reshape(2 * full, model), wide(wh_all)) + shift
             value, slope = gelu_both(pre)
-            act_ref[i, at] = value.astype(BF16).reshape(2, full, units)
+            act_ref[i, at, :, :units] = value.astype(BF16).reshape(2, full, units)
             grad_pre = dot(full_ref[i, at].reshape(2 * full, model), wide(wd_all)) * slope
-            hsum_ref[...] += jnp.sum(grad_pre, axis=0, keepdims=True)
+            hsum[...] += jnp.sum(grad_pre, axis=0, keepdims=True)
             low = grad_pre.astype(BF16)
-            gpl_ref[i, at] = low.reshape(2, full, units)
+            gpl_ref[i, at, :, :units] = low.reshape(2, full, units)
             part_ref[i, at] = dot(low, wide(wh_all), NT).astype(BF16).reshape(2, full, model)
             return 0
 
@@ -729,11 +731,15 @@
     def descend(k, _):
         at = pl.ds(2 * lax.rem(k, 2), 2)
         i = lax.div(k, 2)
-        part = dot(act_ref[i, at].reshape(2 * full, units), wide(wd_all), NT)
+        part = dot(act_ref[i, at, :, :units].reshape(2 * full, units), wide(wd_all), NT)
         two_ref[i, at] = part.astype(BF16).reshape(2, full, model)
         return 0
 
-    totals = [0.0, 0.0, 0.0, 0.0]
+    totals = [0.0] * 6
+
+    def add_up(first, terms):
+        for k, term in enumerate(terms):
+            totals[first + k] = totals[first + k] + jnp.sum(term, axis=0, keepdims=True)
 
     def settle_back(i):
         turns[i].arrive()
@@ -742,12 +748,9 @@
         upper = full_ref[i, me, :rows].astype(F32)
         grad_hidden = upper + norm_backward(grad_normed, unit, inv_std, at_row(gain_two))
         ghid_ref[i] = grad_hidden
-        put[i][7].start()
-        if i < images - 1:
-            one_ref[i, me, :rows] = grad_hidden.astype(BF16)
-            lows[i].start()
-        for k, term in enumerate((grad_normed * unit, grad_normed, grad_hidden, upper)):
-            totals[k] = totals[k] + jnp.sum(term, axis=0, keepdims=True)
+        one_ref[i, me, :rows] = grad_hidden.astype(BF16)
+        lows[i].start()
+        add_up(0, (grad_normed * unit, grad_normed, grad_hidden, upper))
 
     def ready_back(k):
         twos[k].arrive()
@@ -771,233 +774,122 @@
         return 0
 
     lax.fori_loop(0, images, image_back, 0)
+    for step in weights:
+        step.finish()
     outer(gwd_part, full_ref, act_ref, units)
     down.start()
-    for i in range(images - 1):
+    for i in range(last):
         settle_back(i)
     turns[-1].forward()
     down.pair()
     outer(gwh_part, two_ref, gpl_ref, units)
-    put_gwh.start()
-    for step in lows:
-        step.forward()
-    settle_back(images - 1)
+    red_h.start()
+    for i in range(last):
+        lows[i].forward()
     for step in twos:
         step.finish()
     lax.fori_loop(0, 2 * images, descend, 0)
-    for i in range(images):
-        put[i][6].start()
-    for k in range(4):
-        sums_ref[k : k + 1] = totals[k]
-    gwd_ref[...] = down.total()[:, :units]
-    for step, made in zip(lows, put_low):
-        step.arrive()
+    settle_back(last)
+    for step in turns + grads:
+        step.finish()
+    for made in take_one:
         made.start()
-    for step in turns + lows + grads + weights + [down]:
-        step.finish()
-    for i in range(images):
-        for made in put[i][1:]:
-            made.wait()
-    for made in put_low + [put_wq, put_wo, put_gwh]:
-        made.wait()
-
-
-def main(groups, block_input, grad_out, key_mask, vectors, qv_bias, bias, wq, wo, wh, wd):
-    images, rows, model = block_input.shape
-    full = pad_rows(rows)
-    width = wo.shape[1]
-    units = wh.shape[1]
-    heads = width // HD
-    seq = 4 * full
-    depth = wo.shape[0]
-    blocks = ((images, 4, full, model), BF16)
-    own = ((images, rows, model), F32)
-    heads_wide = ((images, heads, seq, 128), BF16)
-    mixed = ((images, 4, full, lanes(width)), BF16)
-    wide = ((images, 4, full, units), BF16)
-    square = ((model, lanes(units)), BF16)
-    weight = lambda count: ((groups, depth, lanes(count)), BF16)
-    outs = [
-        blocks, own, heads_wide, heads_wide, heads_wide, mixed, weight(3 * width), weight(width),
-        ((images - 1, 4, full, model), BF16), own, square, blocks,
-    ]
-    more = [((depth, units), F32), ((4, model), F32), ((1, units), F32)]
-    held = [blocks, blocks, blocks, own, heads_wide, heads_wide, heads_wide, mixed]
-    held += [weight(3 * width), weight(width), weight(units), weight(units)]
-    held += [((heads, seq, HD), BF16), blocks, own, wide, wide, square, square]
-    return pl.pallas_call(
-        functools.partial(main_body, groups, rows, heads),
-        out_shape=tuple(jax.ShapeDtypeStruct(*h) for h in outs + more),
-        in_specs=[VMEM] * 14,
-        out_specs=(ANY,) * len(outs) + (VMEM,) * len(more),
-        scratch_shapes=[pltpu.VMEM(*h) for h in held]
-        + scatter_scratch(images, full, model)
-        + [pltpu.SemaphoreType.DMA((9 * images + 3,))]
-        + reduce_scratch(groups, depth, units)
-        + sems(images, STEPS) * 6
-        + sems(4, groups),
-        compiler_params=params(0),
-        name="main",
-    )(block_input, grad_out, key_mask, *vectors, qv_bias, bias, wq, wo, wh, wd)
-
-
-def close_body(
-    groups, rows, heads,
-    glow_hbm, mixed_hbm, gwh_hbm, mpart_hbm, wo_hbm, qh_hbm, kh_hbm, vh_hbm, wq_hbm, hidden_hbm, ghid_hbm, x_hbm, one_hbm,
-    gain_ref, bias_ref, tsum_ref, hsum_ref,
-    out_ref, gin_ref, gwq_ref, gwo_ref, gwh_ref, both_ref,
-    tok, mixed_ref, gwh_part, mpart_ref, wo_ref, qh, kh, vh, wq_ref, hidden_ref, ghid_ref, x_ref,
-    gq, gk, gv, gh, bsum, gproj, npart, gwq_part, gwo_part, lsem,
-    near, far, passing, near2, far2, passing2,
-    htwin, haway, htsend, htrecv, hfsend, hfrecv,
-    otwin, oaway, otsend, otrecv, ofsend, ofrecv,
-    qtwin, qaway, qtsend, qtrecv, qfsend, qfrecv,
-    mid, msend, mrecv, ssend, srecv, lsend, lrecv, vsend, vrecv, row_in, flat_in,
-):
-    images, _, full, model = tok.shape
-    width = heads * HD
-    seq = 4 * full
-    me, side, over, _ = plane()
-    mine = lax.axis_index("dp")
-    loads = Moves(lsem)
-    held = (
-        (ghid_hbm.at[images - 1], ghid_ref.at[images - 1]), (glow_hbm, tok.at[pl.ds(0, images - 1)]), (wo_hbm, wo_ref),
-        (gwh_hbm, gwh_part), (mpart_hbm, mpart_ref), (qh_hbm, qh), (kh_hbm, kh), (vh_hbm, vh), (mixed_hbm, mixed_ref),
-        (wq_hbm, wq_ref), (hidden_hbm, hidden_ref), (x_hbm, x_ref),
-        (ghid_hbm.at[pl.ds(0, images - 1)], ghid_ref.at[pl.ds(0, images - 1)]),
-    )
-    got = [loads.start(src, dst) for src, dst in held]
-    got_one = loads.plan(one_hbm, tok)
-    bsum[...] = jnp.zeros_like(bsum)
-    outs, sums = [], []
-    for i in range(images):
-        outs.append(Scatter(mpart_ref.at[i], rows, near2.at[i], far2.at[i], passing2.at[i], msend.at[i], mrecv.at[i]))
-        sums.append(Scatter(npart.at[i], rows, near.at[i], far.at[i], passing.at[i], ssend.at[i], srecv.at[i]))
-    red_h = Reduce(groups, gwh_part, htwin, haway, htsend, htrecv, hfsend, hfrecv)
-    red_o = Reduce(groups, gwo_part, otwin, oaway, otsend, otrecv, ofsend, ofrecv)
-    red_q = Reduce(groups, gwq_part, qtwin, qaway, qtsend, qtrecv, qfsend, qfrecv)
-    last = images - 1
-    clear_pads(tok.at[last], rows)
-    low = Gather(tok.at[last], rows, lsend, lrecv)
-    got[0].wait()
-    tok[last, me, :rows] = ghid_ref[last].astype(BF16)
-    greet_all(groups)
-    low.start()
-    for made in got[1:5]:
-        made.wait()
-    red_h.start()
-    for step in outs[:-1]:
-        step.start()
 
     def mix(i):
-        value = dot(tok[i].reshape(seq, model), wo_ref[:, :, :width].reshape(model, width)).astype(BF16)
+        value = dot(one_ref[i].reshape(seq, model), wo_all[:, :, :width].reshape(model, width)).astype(BF16)
+        gpl_ref[i, :, :, 3 * width : 4 * width] = value.reshape(4, full, width)
+
+    def attend_back(i):
         for h in range(heads):
-            gh[i, h] = value[:, h * HD : (h + 1) * HD]
-
-    for i in range(last):
-        mix(i)
-    low.forward()
-    red_h.pair()
-    for made in got[5:]:
-        made.wait()
-    scale = HD**-0.5
-
-    def attend(i):
-        def head(h, _):
+            here = slice(3 * width + h * HD, 3 * width + (h + 1) * HD)
             queries = qh[i, h]
-            grads = gh[i, h]
+            grads_in = gpl_ref[i, :, :, here].reshape(seq, HD)
             keys_in = kh[i, h]
             probs = soft_open(keys_in, queries, scale * LOG2E)
-            grad_probs = dot(vh[i, h, :, :HD], grads, NT)
-            grad_values = dot(probs.astype(BF16), grads)
+            grad_probs = dot(vh[i, h, :, :HD], grads_in, NT)
+            grad_values = dot(probs.astype(BF16), grads_in)
             delta = jnp.sum(probs * grad_probs, axis=0, keepdims=True)
             grad_scores = (probs * (grad_probs - delta) * scale).astype(BF16)
             grad_keys = dot(grad_scores, queries[:, :HD])
             grad_queries = dot(keys_in[:, :HD].T, grad_scores).T
-            for c, (held, value) in enumerate(((gq, grad_queries), (gk, grad_keys), (gv, grad_values))):
-                held[h] = value.astype(BF16)
+            for c, value in enumerate((grad_queries, grad_keys, grad_values)):
+                here = slice(c * width + h * HD, c * width + (h + 1) * HD)
+                gpl_ref[i, :, :, here] = value.astype(BF16).reshape(4, full, HD)
                 bsum[h, c : c + 1] += jnp.sum(value, axis=0, keepdims=True)
-            return 0
-
-        lax.fori_loop(0, heads, head, 0, unroll=4)
-        for h in range(heads):
-            for c, held in enumerate((gq, gk, gv)):
-                at = slice(c * width + h * HD, c * width + (h + 1) * HD)
-                for b in range(4):
-                    gproj[i, b, :, at] = held[h, b * full : (b + 1) * full]
 
     def spread(i):
         def pair(c, _):
             at = pl.ds(2 * c, 2)
-            part = dot(gproj[i, at].reshape(2 * full, 3 * width), wq_ref[:, :, : 3 * width].reshape(model, 3 * width), NT)
-            npart[i, at] = part.astype(BF16).reshape(2, full, model)
+            left = gpl_ref[i, at, :, : 3 * width].reshape(2 * full, 3 * width)
+            part = dot(left, wq_all[:, :, : 3 * width].reshape(model, 3 * width), NT)
+            part_ref[i, at] = part.astype(BF16).reshape(2, full, model)
             return 0
 
         lax.fori_loop(0, 2, pair, 0)
 
-    def between(k):
+    def ready_last(k):
+        lows[k].arrive()
+
+    def send_last(k):
+        if k < last:
+            lows[k + 1].forward()
+        if k > 0:
+            backs[k - 1].forward()
+        backs[k].start()
         if k == 0:
-            for step in outs[:-1]:
-                step.forward()
-
-    def send(k):
-        if k > 0:
-            sums[k - 1].forward()
-        sums[k].start()
-        if k == images - 2:
-            low.arrive()
-            mix(last)
-            outer(gwo_part, tok, mixed_ref, width)
-            red_o.start()
-            low.finish()
-            got_one.start()
-
-    def image(i, _):
-        attend(i)
-        for_image(i, images, between)
+            gwd_ref[...] = down.total()[:, :units]
+            red_h.pair()
+
+    def image_last(i, _):
+        for_image(i, images, ready_last)
+        mix(i)
+        attend_back(i)
         spread(i)
-        for_image(i, images, send)
+        for_image(i, images, send_last)
         return 0
 
-    lax.fori_loop(0, images, image, 0)
+    lax.fori_loop(0, images, image_last, 0)
+    down.finish()
+    outer(gwo_part, one_ref, mixed_ref, width)
+    red_o.start()
+    for made in take_one:
+        made.wait()
+    outer(gwq_part, full_ref, gpl_ref, 3 * width)
     red_o.pair()
-    got_one.wait()
-    outer(gwq_part, tok, gproj, 3 * width)
     red_q.start()
-    totals = [0.0, 0.0]
-
-    def settle(i):
-        sums[i].arrive()
-        grad_normed = sums[i].total(pl.ds(0, rows))
+
+    def settle_last(i):
+        backs[i].arrive()
+        grad_normed = backs[i].total(pl.ds(0, rows))
         unit, inv_std = norm_stats(x_ref[i].astype(F32))
-        gin_ref[i] = ghid_ref[i] + norm_backward(grad_normed, unit, inv_std, at_row(gain_ref))
-        for k, term in enumerate((grad_normed * unit, grad_normed)):
-            totals[k] = totals[k] + jnp.sum(term, axis=0, keepdims=True)
-
-    for i in range(images - 1):
-        settle(i)
-    red_q.pair()
-    sums[-1].forward()
-    outs[-1].start()
+        ghid_ref[i] = ghid_ref[i] + norm_backward(grad_normed, unit, inv_std, at_row(gain_one))
+        put_gin[i].start()
+        add_up(4, (grad_normed * unit, grad_normed))
 
     def finish_out(i):
         outs[i].arrive()
-        out_ref[i] = (hidden_ref[i] + outs[i].total(pl.ds(0, rows)) + at_row(bias_ref)).astype(BF16)
-
-    for i in range(images - 1):
-        finish_out(i)
-    gwh_ref[...] = red_h.total()[:, : gwh_ref.shape[1]]
-    gwo_ref[...] = red_o.total()[:, :width]
+        value = hidden_ref[i] + outs[i].total(pl.ds(0, rows)) + at_row(bias_down)
+        two_ref[i, me, :rows] = value.astype(BF16)
+        put_out[i].start()
+
+    for i in range(last):
+        settle_last(i)
+    backs[-1].forward()
+    for step in outs:
+        step.start()
+    gwh_ref[...] = red_h.total()[:, :units]
+    red_q.pair()
     mid[0] = jnp.zeros_like(mid[0])
-    mid[0, 0:4] = tsum_ref[...]
     for h in range(heads):
         for c in range(3):
             mid[0, 6:7, c * width + h * HD : c * width + (h + 1) * HD] = bsum[h, c : c + 1]
-    mid[0, 7:8, : hsum_ref.shape[1]] = hsum_ref[...]
-    settle(images - 1)
-
-    for k in range(2):
-        mid[0, 4 + k : 5 + k] = totals[k]
+    mid[0, 7:8, :units] = hsum[...]
+    for step in outs[:-1]:
+        step.forward()
+    settle_last(last)
+
+    for k in range(6):
+        mid[0, k : k + 1] = totals[k]
     row_in[mine] = mid[0]
     aways = []
     for k in range(1, groups):
@@ -1016,60 +908,65 @@
         at = groups + k
         planes.append(remote(mid.at[1], flat_in.at[me], vsend.at[at], vrecv.at[at], lax.rem(me + k, 4)))
         planes[-1].start()
+    for i in range(last):
+        finish_out(i)
     for made in planes:
         made.wait()
     both_ref[0:6] = (flat_in[0] + flat_in[1] + flat_in[2] + flat_in[3])[0:6]
     both_ref[6:8] = mid[1, 6:8]
-    finish_out(images - 1)
+    gwo_ref[...] = red_o.total()[:, :width]
+    finish_out(last)
     total = red_q.total()
     for c in range(3):
         gwq_ref[c] = total[:, c * width : (c + 1) * width]
-    for step in sums + outs + [red_h, red_o, red_q]:
+    for step in lows + outs + backs + [red_h, red_o, red_q]:
         step.finish()
-
-
-def close(groups, rows, heads, held, one, gain, bias, tsum, hsum):
-    images, _, full, model = one.shape
-    width = heads * HD
-    units = hsum.shape[1]
-    depth = model // groups
+    for made in put_out + put_gin:
+        made.wait()
+
+
+def whole(groups, block_input, grad_out, key_mask, vectors, qv_bias, bias, wq, wo, wh, wd):
+    images, rows, model = block_input.shape
+    full = pad_rows(rows)
+    width = wo.shape[1]
+    units = wh.shape[1]
+    heads = width // HD
     seq = 4 * full
-    piece = pltpu.VMEM((heads, seq, HD), BF16)
+    depth = wo.shape[0]
+    blocks = ((images, 4, full, model), BF16)
+    own = ((images, rows, model), F32)
+    heads_wide = ((images, heads, seq, 128), BF16)
+    piece = ((heads, seq, HD), BF16)
+    square = ((model, lanes(units)), BF16)
+    weight = lambda count: ((groups, depth, lanes(count)), BF16)
+    outs = [blocks, (block_input.shape, BF16), own]
+    more = [((3, depth, width), F32), ((depth, width), F32), ((depth, units), F32), ((depth, units), F32), ((8, model), F32)]
+    held = [blocks, blocks, blocks, own, heads_wide, heads_wide, heads_wide, ((images, 4, full, lanes(width)), BF16)]
+    held += [weight(3 * width), weight(width), square, square]
+    held += [piece, blocks, own, blocks, blocks, square, square, ((model, lanes(width)), BF16), blocks]
     return pl.pallas_call(
-        functools.partial(close_body, groups, rows, heads),
-        out_shape=(
-            jax.ShapeDtypeStruct((images, rows, model), BF16),
-            jax.ShapeDtypeStruct((images, rows, model), F32),
-            jax.ShapeDtypeStruct((3, depth, width), F32),
-            jax.ShapeDtypeStruct((depth, width), F32),
-            jax.ShapeDtypeStruct((depth, units), F32),
-            jax.ShapeDtypeStruct((8, model), F32),
-        ),
-        in_specs=[ANY] * 13 + [VMEM] * 4,
-        out_specs=(VMEM,) * 6,
-        scratch_shapes=[pltpu.VMEM(h.shape, h.dtype) for h in (one,) + held[1:]]
-        + [piece] * 3
-        + [
-            pltpu.VMEM((images, heads, seq, HD), BF16),
-            pltpu.VMEM((heads, 3, HD), F32),
-            pltpu.VMEM((images, 4, full, 3 * width), BF16),
-            pltpu.VMEM((images, 4, full, model), BF16),
-            pltpu.VMEM((model, lanes(3 * width)), BF16),
-            pltpu.VMEM((model, lanes(width)), BF16),
-            pltpu.SemaphoreType.DMA((14,)),
-        ]
-        + scatter_scratch(images, full, model) * 2
+        functools.partial(whole_body, groups, rows, heads),
+        out_shape=tuple(jax.ShapeDtypeStruct(*h) for h in outs + more),
+        in_specs=[VMEM, ANY] + [VMEM] * 13,
+        out_specs=(ANY,) * len(outs) + (VMEM,) * len(more),
+        scratch_shapes=[pltpu.VMEM(*h) for h in held]
+        + [pltpu.SemaphoreType.DMA((5 * images,))]
         + reduce_scratch(groups, depth, units)
         + reduce_scratch(groups, depth, width)
-        + reduce_scratch(groups, depth, 3 * width)
-        + [pltpu.VMEM((2, 8, model), F32)]
-        + sems(images, STEPS) * 2
-        + sems(STEPS)
-        + sems(groups + 4)
-        + [pltpu.VMEM((groups, 8, model), F32), pltpu.VMEM((4, 8, model), F32)],
-        compiler_params=params(2),
-        name="close",
-    )(*held, one, gain, bias, tsum, hsum)
+        + sems(groups // 2) * 4
+        + sems(8, images, STEPS)
+        + sems(4, groups)
+        + [
+            pltpu.VMEM((1, units), F32),
+            pltpu.VMEM((heads, 3, HD), F32),
+            pltpu.VMEM((2, 8, model), F32),
+            pltpu.VMEM((groups, 8, model), F32),
+            pltpu.VMEM((4, 8, model), F32),
+        ]
+        + sems(groups + 4),
+        compiler_params=params(0),
+        name="whole",
+    )(block_input, grad_out, key_mask, *vectors, qv_bias, bias, wq, wo, wh, wd)
 
 
 def deliver_body(width, out, gin, gwq, gwo, gwh, gwd, both, *refs):
@@ -1128,8 +1025,8 @@
     down_bias,
     grad_out,
 ):
-    flat = ranks == 4
     images, rows, model = block_input.shape
+    flat = ranks == 4 and images == 2 and groups > 2 and groups % 2 == 0 and hidden_weight.shape[1] <= model and 4 * qkv_weight.shape[2] <= lanes(hidden_weight.shape[1])
     seq = key_mask.shape[1]
     width = qkv_weight.shape[2]
     units = hidden_weight.shape[1]
@@ -1142,27 +1039,18 @@
 
     out_rows, down_rows = out_weight.T, down_weight.T
     if flat:
-        (
-            normed_one, hidden_res, qh, kh, vh, mixed, qkv_all, out_all, hidden_full, grad_hidden, hidden_part, mpart,
-            grad_down_w, mlp_sums, unit_sums,
-        ) = main(
+        _, block_output, grad_input, grad_qkv_w, grad_out_w, grad_hidden_w, grad_down_w, both = whole(
             groups,
             block_input,
             grad_out,
             key_mask,
-            (attn_norm_gain, attn_norm_bias, out_bias, mlp_norm_gain, mlp_norm_bias),
+            (attn_norm_gain, attn_norm_bias, out_bias, mlp_norm_gain, mlp_norm_bias, down_bias),
             qv_bias,
             hidden_bias,
             qkv_weight.transpose(1, 0, 2),
             out_rows,
             hidden_weight,
             down_rows,
-        )
-        held = (
-            hidden_full, mixed, hidden_part, mpart, out_all, qh, kh, vh, qkv_all, hidden_res, grad_hidden, block_input
-        )
-        block_output, grad_input, grad_qkv_w, grad_out_w, grad_hidden_w, both = close(
-            groups, rows, width // HD, held, normed_one, attn_norm_gain, down_bias, mlp_sums, unit_sums
         )
         (
             block_output, grad_input, grad_qkv_w, grad_out_w, grad_hidden_w, grad_down_w, grad_qv, grad_hidden_b, *both

time: 278 us -> 267 us (0.960)
  Pallas kernels: 277 us -> 266 us
    pallas_call x2 -> x1, Pallas kernels: 272 us -> 260 us  [whole(): pl.pallas_call(functools.partial(whole_body, groups, rows, heads), out_sh...]
where the time goes in v2:
time: 267 us
  Pallas kernels  266 us (100%)
    pallas_call x1, Pallas kernels, whole(): pl.pallas_call(functools.partial(whole_body, groups, rows, heads), out_sh...  260 us
    pallas_call x1, Pallas kernels, deliver(): pl.pallas_call(functools.partial(deliver_body, width), out_shape=tuple(sa...  5.36 us

profile of v2, /device:TPU:0, one launch (start us, length us, event | category | flops | bytes accessed | tf_op | source)
XLA Modules:
  0.0 266.6 jit_solution(4871556628000450569)
XLA Ops:
  0.7 260.4 %whole.1 = (bf16[2,4,192,1152]{3,2,1,0:T(8,128)(2,1)}, bf16[2,184,1152]{2,1,0:T(8,128)(2,1)}, f32[2,184,1152]{2,1,0:T(8,128)}, f32[3,144,288]{2,1,0:T(8,128)}, f...) custom-call(bf16[2,184,1152]{2,1,0:T(8,128)(2,1)} %x_ref.1, ...), custom_call_target="tpu_custom_call" | custom-call | tf_op jit(solution)/shard_map/whole/pallas_call | solution.py:947
  261.1 5.4 %deliver.1 = (bf16[2,184,1152]{2,1,0:T(8,128)(2,1)}, f32[2,184,1152]{2,1,0:T(8,128)}, f32[3,144,288]{2,1,0:T(8,128)}, f32[144,288]{1,0:T(8,128)}, f32[144,1076]{...) custom-call(bf16[2,184,1152]{2,1,0:T(8,128)(2,1)} %get-tuple-element, ...), custom_call_target="tpu_custom_call" | custom-call | tf_op jit(solution)/shard_map/deliver/pallas_call | solution.py:990

commit v3 on v2

--- a/solution.py
+++ b/solution.py
@@ -209,13 +209,14 @@
     pl.semaphore_wait(barrier, len(peers))
 
 
-def greet_all(groups):
+def greet_all(groups, work):
     row, me = lax.axis_index("dp"), lax.axis_index("tensor")
     barrier = pltpu.get_barrier_semaphore()
     peers = [{"dp": lax.rem(row + k, groups)} for k in range(1, groups)]
     peers += [{"tensor": lax.rem(me + k, 4)} for k in range(1, 4)]
     for peer in peers:
         pl.semaphore_signal(barrier, inc=1, device_id=peer, device_id_type=MESH)
+    work()
     pl.semaphore_wait(barrier, len(peers))
 
 
@@ -261,8 +262,8 @@
             self.copies[k].wait_recv()
             self.copies[4 + k].start()
 
-    def arrive(self):
-        for made in self.copies[2:]:
+    def arrive(self, first=2, last=6):
+        for made in self.copies[first:last]:
             made.wait_recv()
 
     def finish(self):
@@ -509,19 +510,16 @@
     return [pltpu.VMEM((half, depth, width), BF16), pltpu.VMEM((half - 1, depth, width), BF16)] + sems(half) * 2
 
 
-def outer(out_ref, left_ref, right_ref, width):
+def outer(out_ref, left_ref, right_ref, width, first=0):
     images, blocks, full, model = left_ref.shape
     count = images * blocks * full
     tile = 384
-    extra = out_ref.shape[1] - width
-    if extra > 0:
-        out_ref[:, width:] = jnp.zeros((out_ref.shape[0], extra), BF16)
 
     def part(c, _):
         at = pl.ds(pl.multiple_of(c * tile, tile), tile)
         left = left_ref[:, :, :, at].reshape(count, tile)
         right = right_ref[:, :, :, :width].reshape(count, width)
-        out_ref[at, :width] = dot(left, right, TN).astype(BF16)
+        out_ref[at, first : first + width] = dot(left, right, TN).astype(BF16)
         return 0
 
     lax.fori_loop(0, model // tile, part, 0)
@@ -533,10 +531,10 @@
     wq_ref, wo_ref, wh_ref, wd_ref,
     one_out, block_out, gin_out, gwq_ref, gwo_ref, gwh_ref, gwd_ref, both_ref,
     one_ref, full_ref, two_ref, hidden_ref, qh, kh, vh, mixed_ref, wq_all, wo_all, wh_all, wd_all,
-    gq, part_ref, ghid_ref, act_ref, gpl_ref, gwh_part, gwd_part, gwo_part, slots, osem,
+    gq, part_ref, ghid_ref, act_ref, gpl_ref, gwh_part, gwd_part, slots, osem,
     dtwin, daway, dtsend, dtrecv, dfsend, dfrecv,
-    otwin, oaway, otsend, otrecv, ofsend, ofrecv,
-    htsend, htrecv, hfsend, hfrecv, qtsend, qtrecv, qfsend, qfrecv,
+    htwin, haway, htsend, htrecv, hfsend, hfrecv,
+    qtsend, qtrecv, qfsend, qfrecv,
     gsend, grecv, wsend, wrecv,
     hsum, bsum, mid, row_in, flat_in, vsend, vrecv,
 ):
@@ -575,26 +573,21 @@
         outs.append(Scatter(two_ref.at[i], rows, spare, *pair(6)))
         backs.append(Scatter(part_ref.at[i], rows, four, *pair(7)))
     down = Reduce(groups, gwd_part, dtwin, daway, dtsend, dtrecv, dfsend, dfrecv)
-    red_h = Reduce(groups, gwh_part, wh_all.at[:, pl.ds(0, lanes(units))], None, htsend, htrecv, hfsend, hfrecv)
-    red_o = Reduce(groups, gwo_part, otwin, oaway, otsend, otrecv, ofsend, ofrecv)
-    gwq_part = gwd_part.at[:, pl.ds(0, lanes(3 * width))]
-    red_q = Reduce(groups, gwq_part, wd_all.at[:, pl.ds(0, lanes(3 * width))], None, qtsend, qtrecv, qfsend, qfrecv)
+    red_h = Reduce(groups, gwh_part, htwin, haway, htsend, htrecv, hfsend, hfrecv)
+    red_q = Reduce(groups, gwd_part, wd_all, None, qtsend, qtrecv, qfsend, qfrecv)
     moves = Moves(osem)
     keep_one = [moves.plan(one_ref.at[i], one_out.at[i]) for i in range(images)]
     take_one = [moves.plan(one_out.at[i], full_ref.at[i]) for i in range(images)]
     take_grad = [moves.plan(grad_ref.at[i], full_ref.at[i, me, pl.ds(0, rows)]) for i in range(images)]
+    put_out = [moves.plan(two_ref.at[i, me, pl.ds(0, rows)], block_out.at[i]) for i in range(images)]
+    put_gin = [moves.plan(ghid_ref.at[i], gin_out.at[i]) for i in range(images)]
+
+    def enter(i):
+        one_ref[i, me, :rows] = norm_forward(x_ref[i].astype(F32), at_row(gain_one), at_row(bias_one))
+
     for made in take_grad:
         made.start()
-    put_out = [moves.plan(two_ref.at[i, me, pl.ds(0, rows)], block_out.at[i]) for i in range(images)]
-    put_gin = [moves.plan(ghid_ref.at[i], gin_out.at[i]) for i in range(images)]
-
-    def enter(i):
-        one_ref[i, me, :rows] = norm_forward(x_ref[i].astype(F32), at_row(gain_one), at_row(bias_one))
-
-    enter(0)
-    for made in take_grad:
-        made.wait()
-    greet_all(groups)
+    greet_all(groups, lambda: enter(0))
     ones[0].start()
     wq.start()
     for i in range(1, images):
@@ -613,6 +606,8 @@
             qh[i, h, :, HD:] = tail
     for step in ones:
         step.forward()
+    for made in take_grad:
+        made.wait()
     grads[0].start()
     wq.hop()
     wq.forward()
@@ -665,7 +660,6 @@
 
     def between(k):
         if k == 0:
-            grads[0].forward()
             wo.hop()
             wo.forward()
             wh.hop()
@@ -675,6 +669,8 @@
         if k > 0:
             sums[k - 1].forward()
         sums[k].start()
+        if k == 0:
+            grads[0].forward()
 
     def image(i, _):
         for_image(i, images, ready)
@@ -701,11 +697,11 @@
     for i in range(last):
         twos[i].forward()
     settle(last)
-    for step in grads[1:]:
-        step.start()
     wh.forward()
     wd.forward()
     twos[-1].forward()
+    for step in grads[1:]:
+        step.start()
     for step in sums + ones:
         step.finish()
     for made in keep_one:
@@ -776,20 +772,23 @@
     lax.fori_loop(0, images, image_back, 0)
     for step in weights:
         step.finish()
+    gwd_part[:, units:] = jnp.zeros((model, lanes(units) - units), BF16)
     outer(gwd_part, full_ref, act_ref, units)
     down.start()
     for i in range(last):
         settle_back(i)
     turns[-1].forward()
     down.pair()
+    gwh_part[:, units:] = jnp.zeros((model, lanes(units) - units), BF16)
     outer(gwh_part, two_ref, gpl_ref, units)
-    red_h.start()
     for i in range(last):
         lows[i].forward()
     for step in twos:
         step.finish()
     lax.fori_loop(0, 2 * images, descend, 0)
+    red_h.start()
     settle_back(last)
+    red_h.pair()
     for step in turns + grads:
         step.finish()
     for made in take_one:
@@ -799,8 +798,16 @@
         value = dot(one_ref[i].reshape(seq, model), wo_all[:, :, :width].reshape(model, width)).astype(BF16)
         gpl_ref[i, :, :, 3 * width : 4 * width] = value.reshape(4, full, width)
 
+    def midway(k):
+        if k < last:
+            lows[k + 1].forward()
+        if k > 0:
+            backs[k - 1].forward()
+
     def attend_back(i):
         for h in range(heads):
+            if h == heads // 2:
+                for_image(i, images, midway)
             here = slice(3 * width + h * HD, 3 * width + (h + 1) * HD)
             queries = qh[i, h]
             grads_in = gpl_ref[i, :, :, here].reshape(seq, HD)
@@ -828,17 +835,15 @@
         lax.fori_loop(0, 2, pair, 0)
 
     def ready_last(k):
-        lows[k].arrive()
+        lows[k].arrive(4 if k > 0 else 2)
 
     def send_last(k):
+        backs[k].start()
         if k < last:
-            lows[k + 1].forward()
-        if k > 0:
-            backs[k - 1].forward()
-        backs[k].start()
-        if k == 0:
-            gwd_ref[...] = down.total()[:, :units]
-            red_h.pair()
+            lows[k + 1].arrive(2, 4)
+            outs[k].start()
+        else:
+            outs[k - 1].forward()
 
     def image_last(i, _):
         for_image(i, images, ready_last)
@@ -849,13 +854,12 @@
         return 0
 
     lax.fori_loop(0, images, image_last, 0)
+    gwd_ref[...] = down.total()[:, :units]
     down.finish()
-    outer(gwo_part, one_ref, mixed_ref, width)
-    red_o.start()
+    outer(gwd_part, one_ref, mixed_ref, width, 3 * width)
     for made in take_one:
         made.wait()
-    outer(gwq_part, full_ref, gpl_ref, 3 * width)
-    red_o.pair()
+    outer(gwd_part, full_ref, gpl_ref, 3 * width)
     red_q.start()
 
     def settle_last(i):
@@ -875,8 +879,7 @@
     for i in range(last):
         settle_last(i)
     backs[-1].forward()
-    for step in outs:
-        step.start()
+    outs[-1].start()
     gwh_ref[...] = red_h.total()[:, :units]
     red_q.pair()
     mid[0] = jnp.zeros_like(mid[0])
@@ -884,8 +887,6 @@
         for c in range(3):
             mid[0, 6:7, c * width + h * HD : c * width + (h + 1) * HD] = bsum[h, c : c + 1]
     mid[0, 7:8, :units] = hsum[...]
-    for step in outs[:-1]:
-        step.forward()
     settle_last(last)
 
     for k in range(6):
@@ -914,12 +915,12 @@
         made.wait()
     both_ref[0:6] = (flat_in[0] + flat_in[1] + flat_in[2] + flat_in[3])[0:6]
     both_ref[6:8] = mid[1, 6:8]
-    gwo_ref[...] = red_o.total()[:, :width]
     finish_out(last)
     total = red_q.total()
     for c in range(3):
         gwq_ref[c] = total[:, c * width : (c + 1) * width]
-    for step in lows + outs + backs + [red_h, red_o, red_q]:
+    gwo_ref[...] = total[:, 3 * width : 4 * width]
+    for step in lows + outs + backs + [red_h, red_q]:
         step.finish()
     for made in put_out + put_gin:
         made.wait()
@@ -943,7 +944,7 @@
     more = [((3, depth, width), F32), ((depth, width), F32), ((depth, units), F32), ((depth, units), F32), ((8, model), F32)]
     held = [blocks, blocks, blocks, own, heads_wide, heads_wide, heads_wide, ((images, 4, full, lanes(width)), BF16)]
     held += [weight(3 * width), weight(width), square, square]
-    held += [piece, blocks, own, blocks, blocks, square, square, ((model, lanes(width)), BF16), blocks]
+    held += [piece, blocks, own, blocks, blocks, square, square, blocks]
     return pl.pallas_call(
         functools.partial(whole_body, groups, rows, heads),
         out_shape=tuple(jax.ShapeDtypeStruct(*h) for h in outs + more),
@@ -951,9 +952,8 @@
         out_specs=(ANY,) * len(outs) + (VMEM,) * len(more),
         scratch_shapes=[pltpu.VMEM(*h) for h in held]
         + [pltpu.SemaphoreType.DMA((5 * images,))]
-        + reduce_scratch(groups, depth, units)
-        + reduce_scratch(groups, depth, width)
-        + sems(groups // 2) * 4
+        + reduce_scratch(groups, depth, units) * 2
+        + sems(groups // 2) * 2
         + sems(8, images, STEPS)
         + sems(4, groups)
         + [
@@ -970,17 +970,20 @@
 
 
 def deliver_body(width, out, gin, gwq, gwo, gwh, gwd, both, *refs):
-    refs, sem = refs[:-1], refs[-1]
-    loads = Moves(sem)
-    for src, dst in zip((out, gin, gwq, gwo, gwh, gwd), refs):
-        loads.start(src, dst)
+    refs, held, lsem, ssem = refs[:14], refs[14:20], refs[20], refs[21]
+    loads, stores = Moves(lsem), Moves(ssem)
+    sources = (out, gin, gwq, gwo, gwh, gwd)
+    got = [loads.start(src, mid) for src, mid in zip(sources, held)]
     qv, unit = refs[6:8]
     qv[0:1] = both[6:7, :width]
     qv[1:2] = both[6:7, 2 * width : 3 * width]
     unit[...] = both[7, : unit.shape[0]]
     for k, dst in enumerate(refs[8:]):
         dst[...] = both[k]
-    loads.finish()
+    for made, mid, dst in zip(got, held, refs):
+        made.wait()
+        stores.start(mid, dst)
+    stores.finish()
 
 
 def deliver(width, units, out, gin, gwq, gwo, gwh, gwd, both):
@@ -991,8 +994,9 @@
         functools.partial(deliver_body, width),
         out_shape=tuple(same + more),
         in_specs=[ANY] * 6 + [VMEM],
-        out_specs=(VMEM,) * 14,
-        scratch_shapes=[pltpu.SemaphoreType.DMA((6,))],
+        out_specs=(ANY,) * 6 + (VMEM,) * 8,
+        scratch_shapes=[pltpu.VMEM(v.shape, v.dtype) for v in same]
+        + [pltpu.SemaphoreType.DMA((6,)), pltpu.SemaphoreType.DMA((6,))],
         compiler_params=pltpu.CompilerParams(vmem_limit_bytes=60 << 20),
         name="deliver",
     )(out, gin, gwq, gwo, gwh, gwd, both)
@@ -1026,7 +1030,7 @@
     grad_out,
 ):
     images, rows, model = block_input.shape
-    flat = ranks == 4 and images == 2 and groups > 2 and groups % 2 == 0 and hidden_weight.shape[1] <= model and 4 * qkv_weight.shape[2] <= lanes(hidden_weight.shape[1])
+    flat = ranks == 4 and images == 2 and groups > 2 and groups % 2 == 0 and hidden_weight.shape[1] <= model and 4 * qkv_weight.shape[2] == lanes(hidden_weight.shape[1])
     seq = key_mask.shape[1]
     width = qkv_weight.shape[2]
     units = hidden_weight.shape[1]

time: 267 us -> 261 us (0.978)
  Pallas kernels: 266 us -> 260 us
    pallas_call x1, Pallas kernels: 260 us -> 255 us  [whole(): pl.pallas_call(functools.partial(whole_body, groups, rows, heads), out_sh...]
where the time goes in v3:
time: 261 us
  Pallas kernels  260 us (100%)
    pallas_call x1, Pallas kernels, whole(): pl.pallas_call(functools.partial(whole_body, groups, rows, heads), out_sh...  255 us

profile of v3, /device:TPU:0, one launch (start us, length us, event | category | flops | bytes accessed | tf_op | source)
XLA Modules:
  0.0 261.0 jit_solution(11660195602340163384)
XLA Ops:
  0.7 255.0 %whole.1 = (bf16[2,4,192,1152]{3,2,1,0:T(8,128)(2,1)}, bf16[2,184,1152]{2,1,0:T(8,128)(2,1)}, f32[2,184,1152]{2,1,0:T(8,128)}, f32[3,144,288]{2,1,0:T(8,128)}, f...) custom-call(bf16[2,184,1152]{2,1,0:T(8,128)(2,1)} %x_ref.1, ...), custom_call_target="tpu_custom_call" | custom-call | tf_op jit(solution)/shard_map/whole/pallas_call | solution.py:948
  255.7 5.1 %deliver.1 = (bf16[2,184,1152]{2,1,0:T(8,128)(2,1)}, f32[2,184,1152]{2,1,0:T(8,128)}, f32[3,144,288]{2,1,0:T(8,128)}, f32[144,288]{1,0:T(8,128)}, f32[144,1076]{...) custom-call(bf16[2,184,1152]{2,1,0:T(8,128)(2,1)} %get-tuple-element, ...), custom_call_target="tpu_custom_call" | custom-call | tf_op jit(solution)/shard_map/deliver/pallas_call | solution.py:993

commit v4 on v3

--- a/solution.py
+++ b/solution.py
@@ -608,7 +608,8 @@
         step.forward()
     for made in take_grad:
         made.wait()
-    grads[0].start()
+    for step in grads:
+        step.start()
     wq.hop()
     wq.forward()
     scale = HD**-0.5
@@ -669,8 +670,7 @@
         if k > 0:
             sums[k - 1].forward()
         sums[k].start()
-        if k == 0:
-            grads[0].forward()
+        grads[k].forward()
 
     def image(i, _):
         for_image(i, images, ready)
@@ -697,11 +697,9 @@
     for i in range(last):
         twos[i].forward()
     settle(last)
+    twos[-1].forward()
     wh.forward()
     wd.forward()
-    twos[-1].forward()
-    for step in grads[1:]:
-        step.start()
     for step in sums + ones:
         step.finish()
     for made in keep_one:
@@ -756,9 +754,6 @@
         grads[k].arrive()
 
     def send_back(k):
-        if k == 0:
-            for step in grads[1:]:
-                step.forward()
         if k > 0:
             turns[k - 1].forward()
         turns[k].start()

time: 261 us -> 258 us (0.989)
  Pallas kernels: 260 us -> 256 us
    pallas_call x1, Pallas kernels: 255 us -> 251 us  [whole(): pl.pallas_call(functools.partial(whole_body, groups, rows, heads), out_sh...]
where the time goes in v4:
time: 258 us; the launch traced here: 257 us
  Pallas kernels  256 us (99%)
    pallas_call x1, Pallas kernels, whole(): pl.pallas_call(functools.partial(whole_body, groups, rows, heads), out_sh...  251 us

profile of v4, /device:TPU:0, one launch (start us, length us, event | category | flops | bytes accessed | tf_op | source)
XLA Modules:
  0.0 257.3 jit_solution(9706947862168440906)
XLA Ops:
  0.7 251.4 %whole.1 = (bf16[2,4,192,1152]{3,2,1,0:T(8,128)(2,1)}, bf16[2,184,1152]{2,1,0:T(8,128)(2,1)}, f32[2,184,1152]{2,1,0:T(8,128)}, f32[3,144,288]{2,1,0:T(8,128)}, f...) custom-call(bf16[2,184,1152]{2,1,0:T(8,128)(2,1)} %x_ref.1, ...), custom_call_target="tpu_custom_call" | custom-call | tf_op jit(solution)/shard_map/whole/pallas_call | solution.py:943
  252.0 5.1 %deliver.1 = (bf16[2,184,1152]{2,1,0:T(8,128)(2,1)}, f32[2,184,1152]{2,1,0:T(8,128)}, f32[3,144,288]{2,1,0:T(8,128)}, f32[144,288]{1,0:T(8,128)}, f32[144,1076]{...) custom-call(bf16[2,184,1152]{2,1,0:T(8,128)(2,1)} %get-tuple-element, ...), custom_call_target="tpu_custom_call" | custom-call | tf_op jit(solution)/shard_map/deliver/pallas_call | solution.py:988

commit v5 on v4

--- a/solution.py
+++ b/solution.py
@@ -838,6 +838,7 @@
             lows[k + 1].arrive(2, 4)
             outs[k].start()
         else:
+            outs[k].start()
             outs[k - 1].forward()
 
     def image_last(i, _):
@@ -874,7 +875,6 @@
     for i in range(last):
         settle_last(i)
     backs[-1].forward()
-    outs[-1].start()
     gwh_ref[...] = red_h.total()[:, :units]
     red_q.pair()
     mid[0] = jnp.zeros_like(mid[0])

time: 258 us -> 258 us (level)
  no operation moved by 1% of the time
where the time goes in v5:
time: 258 us; the launch traced here: 257 us
  Pallas kernels  256 us (99%)
    pallas_call x1, Pallas kernels, whole(): pl.pallas_call(functools.partial(whole_body, groups, rows, heads), out_sh...  251 us

profile of v5, /device:TPU:0, one launch (start us, length us, event | category | flops | bytes accessed | tf_op | source)
XLA Modules:
  0.0 257.3 jit_solution(13000513361260330113)
XLA Ops:
  0.7 251.3 %whole.1 = (bf16[2,4,192,1152]{3,2,1,0:T(8,128)(2,1)}, bf16[2,184,1152]{2,1,0:T(8,128)(2,1)}, f32[2,184,1152]{2,1,0:T(8,128)}, f32[3,144,288]{2,1,0:T(8,128)}, f...) custom-call(bf16[2,184,1152]{2,1,0:T(8,128)(2,1)} %x_ref.1, ...), custom_call_target="tpu_custom_call" | custom-call | tf_op jit(solution)/shard_map/whole/pallas_call | solution.py:943
  252.0 5.1 %deliver.1 = (bf16[2,184,1152]{2,1,0:T(8,128)(2,1)}, f32[2,184,1152]{2,1,0:T(8,128)}, f32[3,144,288]{2,1,0:T(8,128)}, f32[144,288]{1,0:T(8,128)}, f32[144,1076]{...) custom-call(bf16[2,184,1152]{2,1,0:T(8,128)(2,1)} %get-tuple-element, ...), custom_call_target="tpu_custom_call" | custom-call | tf_op jit(solution)/shard_map/deliver/pallas_call | solution.py:988
